TPU v7x, 32 devices: a 4x4x1 block of a 4x4x8 slice. The times are simulated.
32 devices in a mesh: part: 1 (over z), tp: 4 (over y), ep: 8 (over x, core).
Axes of the slice: x: 4, y: 4, z: 1, core: 2. Of those that a mesh axis runs over, the one named last changes fastest.
The devices are a block of a 4x4x8 slice.
Arguments:
- dec_states: bfloat16 [64, 512, 768], P(('part', 'ep'))
- enc_states: bfloat16 [64, 256, 768], P(('part', 'ep'))
- enc_pad: int32 [64, 256], P(('part', 'ep'))
- expert_idx: int32 [64, 512], P(('part', 'ep'))
- self_bias: float32 [12, 512, 512], P('tp')
- gain_self: float32 [768], replicated
- wq_self: bfloat16 [768, 768], P(None, 'tp')
- wk_self: bfloat16 [768, 768], P(None, 'tp')
- wv_self: bfloat16 [768, 768], P(None, 'tp')
- wo_self: bfloat16 [768, 768], P('tp')
- gain_cross: float32 [768], replicated
- wq_cross: bfloat16 [768, 768], P(None, 'tp')
- wk_cross: bfloat16 [768, 768], P(None, 'tp')
- wv_cross: bfloat16 [768, 768], P(None, 'tp')
- wo_cross: bfloat16 [768, 768], P('tp')
- gain_ffn: float32 [768], replicated
- w_router: float32 [768, 128], replicated
- w_in: bfloat16 [128, 768, 3072], P('ep')
- w_out: bfloat16 [128, 3072, 768], P('ep')
Outputs:
- output: bfloat16 [64, 512, 768], P(('part', 'ep'))
All inputs are finite; a program needn't handle non-finite values.
Results may differ from a plain program's by a relative error of at most 0.02.
Values are sent between devices in bfloat16 or wider.
A program may use at most 768 MiB of HBM per device.

v0:
```python
import jax
import jax.numpy as jnp
from jax import lax
from jax.sharding import PartitionSpec as P

EPSILON = 1e-6
NEG_LARGE = -1e30


def rms_norm(states, gain_vec):
    upcast = states.astype(jnp.float32)
    mean_sq = jnp.mean(upcast * upcast, axis=-1, keepdims=True)
    return (upcast * lax.rsqrt(mean_sq + EPSILON) * gain_vec).astype(jnp.bfloat16)


def head_project(states, weight, heads):
    projected = jnp.einsum('bld,dk->blk', states, weight, preferred_element_type=jnp.float32)
    return projected.astype(jnp.bfloat16).reshape(states.shape[0], states.shape[1], heads, weight.shape[1] // heads)


def attention_heads(normed, source, bias_mask, w_query, w_key, w_value, w_output, heads):
    queries = head_project(normed, w_query, heads)
    key_heads = head_project(source, w_key, heads)
    values = head_project(source, w_value, heads)
    scores = jnp.einsum('bqhe,bkhe->bhqk', queries, key_heads, preferred_element_type=jnp.float32) + bias_mask
    weights = jax.nn.softmax(scores, axis=-1).astype(jnp.bfloat16)
    context = jnp.einsum('bhqk,bkhe->bhqe', weights, values, preferred_element_type=jnp.float32).astype(jnp.bfloat16)
    w_heads = w_output.reshape(heads, w_output.shape[0] // heads, w_output.shape[1])
    return jnp.einsum('cirf,ife->cre', context, w_heads, preferred_element_type=jnp.float32)


def router_choice(normed, choice, w_router):
    tokens, experts = normed.shape[0], w_router.shape[1]
    logits = jnp.dot(normed, w_router, precision=lax.Precision.HIGHEST, preferred_element_type=jnp.float32)
    router_prob = jax.nn.softmax(logits, axis=-1)
    one_hot = (choice[:, None] == lax.broadcasted_iota(jnp.int32, (tokens, experts), 1)).astype(jnp.int32)
    gate_prob = jnp.sum(router_prob * one_hot, axis=-1)
    position = jnp.sum((jnp.cumsum(one_hot, axis=0) - 1) * one_hot, axis=-1)
    return gate_prob, position


def expert_layer(states, expert_idx, gain_ffn, w_router, w_in, w_out, ep_size):
    batch_dev, dec_len, d_model = states.shape
    tokens = batch_dev * dec_len
    experts = w_router.shape[1]
    capacity = (5 * tokens + 4 * experts - 1) // (4 * experts)
    normed = rms_norm(states, gain_ffn).reshape(tokens, d_model)
    choice = expert_idx.reshape(tokens)
    gate_prob, position = router_choice(normed, choice, w_router)
    slot_id = jnp.where(position < capacity, choice * capacity + position, -1)
    dispatch = (slot_id[:, None] == lax.broadcasted_iota(jnp.int32, (tokens, experts * capacity), 1)).astype(jnp.bfloat16)
    send_buf = jnp.einsum('sc,sd->cd', dispatch, normed, preferred_element_type=jnp.float32).astype(jnp.bfloat16)
    received = lax.all_to_all(send_buf.reshape(experts, capacity, d_model), 'ep', 0, 0, tiled=True)
    received = received.reshape(ep_size, experts // ep_size, capacity, d_model)
    hidden = jnp.maximum(jnp.einsum('gecd,edf->gecf', received, w_in, preferred_element_type=jnp.float32), 0.0).astype(jnp.bfloat16)
    expert_out = jnp.einsum('gecf,efd->gecd', hidden, w_out, preferred_element_type=jnp.float32).astype(jnp.bfloat16)
    returned = lax.all_to_all(expert_out.reshape(experts, capacity, d_model), 'ep', 0, 0, tiled=True)
    combined = jnp.einsum('sc,cd->sd', dispatch, returned.reshape(experts * capacity, d_model), preferred_element_type=jnp.float32)
    result = states.reshape(tokens, d_model).astype(jnp.float32) + gate_prob[:, None] * combined
    return result.astype(jnp.bfloat16).reshape(batch_dev, dec_len, d_model)


def solution(mesh):
    ep_size = mesh.shape['ep']
    token_spec = P(('part', 'ep'), None, None)
    row_spec = P(('part', 'ep'), None)
    col_spec = P(None, 'tp')
    head_rows = P('tp', None)
    vec_spec = P(None)
    expert_spec = P('ep', None, None)
    in_specs = (token_spec, token_spec, row_spec, row_spec, P('tp', None, None), vec_spec, col_spec, col_spec, col_spec, head_rows, vec_spec, col_spec, col_spec, col_spec, head_rows, vec_spec, P(None, None), expert_spec, expert_spec)

    def layer(dec_states, enc_states, enc_pad, expert_idx, self_bias, gain_self, wq_self, wk_self, wv_self, wo_self, gain_cross, wq_cross, wk_cross, wv_cross, wo_cross, gain_ffn, w_router, w_in, w_out):
        dec_len = dec_states.shape[1]
        local_heads = self_bias.shape[0]
        row_ids = lax.broadcasted_iota(jnp.int32, (dec_len, dec_len), 0)
        col_ids = lax.broadcasted_iota(jnp.int32, (dec_len, dec_len), 1)
        causal_bias = jnp.where(col_ids <= row_ids, self_bias, NEG_LARGE)[None]
        normed = rms_norm(dec_states, gain_self)
        partial = attention_heads(normed, normed, causal_bias, wq_self, wk_self, wv_self, wo_self, local_heads)
        attn_sum = lax.psum(partial.astype(jnp.bfloat16), 'tp')
        after_self = (dec_states.astype(jnp.float32) + attn_sum.astype(jnp.float32)).astype(jnp.bfloat16)
        pad_bias = jnp.where(enc_pad == 0, 0.0, NEG_LARGE).astype(jnp.float32)[:, None, None, :]
        normed = rms_norm(after_self, gain_cross)
        partial = attention_heads(normed, enc_states, pad_bias, wq_cross, wk_cross, wv_cross, wo_cross, local_heads)
        attn_sum = lax.psum(partial.astype(jnp.bfloat16), 'tp')
        after_cross = (after_self.astype(jnp.float32) + attn_sum.astype(jnp.float32)).astype(jnp.bfloat16)
        return expert_layer(after_cross, expert_idx, gain_ffn, w_router, w_in, w_out, ep_size)

    return jax.shard_map(layer, mesh=mesh, in_specs=in_specs, out_specs=token_spec, check_vma=False)
```

profile of v0, /device:TPU:97, one launch (start us, length us, event | category | flops | bytes accessed | tf_op | source)
XLA Modules:
  0.0 722.9 jit_solution(6565690562266498647)
XLA Ops:
  6.5 0.0 copy-start
  6.6 0.0 all-reduce.3.cloned.1.call-start
  6.6 0.0 copy-start.3
  6.6 0.1 iota_compare_fusion.10
  6.7 4.2 fusion.16
  10.9 0.5 copy-done.3
  11.4 3.5 fusion.60
  15.0 3.6 fusion.63
  18.6 3.6 fusion.57
  22.2 2.2 broadcast_select_fusion
  24.3 3.6 copy.23
  28.0 15.1 %fusion.81 = (f32[8,3,512]{2,1,0:T(4,128)S(1)}, f32[8,3,512,512]{2,3,1,0:T(8,128)}) fusion(f32[3,512,512]{1,2,0:T(8,128)} %copy.23, bf16[8,512,3,64]{1,3,2,0:T(8,128)(2,1)} %bitcast.113, bf16[8,512,3,64]{1,3,2,0:T(8,128)(2,1)} %bitcast.112), kind=kOutput, calls=%fused_computation.93 | convolution fusion | flops 824181248 | bytes 31506432 | tf_op jit(solution)/shard_map/sub | solution.py:26
  43.0 13.6 %bitcast_convert_fusion.1 = bf16[8,512,768]{2,1,0:T(8,128)(2,1)} fusion(bf16[3,64,768,1]{2,1,0,3:T(8,128)(2,1)S(1)} %bitcast.118, bf16[8,512,3,64]{1,3,2,0:T(8,128)(2,1)} %bitcast.120, f32[8,3,512,512]{2,3,1,0:T(8,128)} %get-tuple-element.10, f32[8,3,512]{2,1,0:T(4,128)S(1)} %get-tuple-element.9), kind=kOutput, calls=%fused_computation.35 | convolution fusion | flops 2029780992 | bytes 33374208 | tf_op jit(solution)/shard_map/cirf,ife->cre/dot_general | solution.py:29
  56.7 0.1 all-reduce.3.cloned.1.call-update
  56.7 0.3 all-reduce.5.cloned.1.call-start
  57.0 0.4 copy-done.9
  57.4 0.1 copy.24
  57.5 0.1 copy-done.18
  57.7 2.1 convolution_convert_fusion.1
  59.7 3.1 convolution_convert_fusion
  62.8 119.4 %all-reduce.3.cloned.1.call-done = bf16[8,512,768]{2,1,0:T(8,128)(2,1)} async-done(((bf16[8,512,768]{2,1,0:T(8,128)(2,1)}), bf16[8,512,768]{2,1,0:T(8,128)(2,1)}) %all-reduce.3.cloned.1.call-update) | async-done | bytes 6291472 | tf_op jit(solution)/shard_map/psum | solution.py:81
  182.2 9.5 %fusion.20 = (f32[8,512]{1,0:T(8,128)S(1)}, bf16[8,512,768]{2,1,0:T(8,128)(2,1)}) fusion(bf16[8,512,768]{2,1,0:T(8,128)(2,1)} %all-reduce.3.cloned.1.call-done, bf16[8,512,768]{2,1,0:T(8,128)(2,1)} %param.19), kind=kLoop, calls=%fused_computation.28 | loop fusion | flops 22016000 | bytes 18890752 | tf_op jit(solution)/shard_map/reduce_sum | solution.py:12
  191.7 5.1 fusion.66
  196.8 0.0 copy-start.20
  196.9 0.0 copy-start.23
  196.9 9.9 %fusion.82 = (f32[8,3,512]{2,1,0:T(4,128)S(1)}, f32[8,3,512,256]{2,3,1,0:T(8,128)}) fusion(f32[8,256]{1,0:T(8,128)S(1)} %compare_select_fusion, bf16[8,512,3,64]{1,3,2,0:T(8,128)(2,1)S(1)} %bitcast.121, bf16[8,256,3,64]{1,3,2,0:T(8,128)(2,1)} %bitcast.123), kind=kOutput, calls=%fused_computation.94 | convolution fusion | flops 412090624 | bytes 14999552 | tf_op jit(solution)/shard_map/sub | solution.py:26
  206.8 10.6 %bitcast_convert_fusion = bf16[8,512,768]{2,1,0:T(8,128)(2,1)} fusion(bf16[3,64,768,1]{2,1,0,3:T(8,128)(2,1)S(1)} %bitcast.119, bf16[8,256,3,64]{1,3,2,0:T(8,128)(2,1)S(1)} %bitcast.122, f32[8,3,512,256]{2,3,1,0:T(8,128)} %get-tuple-element.12, f32[8,3,512]{2,1,0:T(4,128)S(1)} %get-tuple-element.11), kind=kOutput, calls=%fused_computation.34 | convolution fusion | flops 1620836352 | bytes 20004864 | tf_op jit(solution)/shard_map/cirf,ife->cre/dot_general | solution.py:29
  217.5 0.1 all-reduce.5.cloned.1.call-update
  217.5 0.6 fusion.53
  218.1 0.1 reduce-window.9
  218.2 1.6 add_add_fusion
  219.8 2.7 copy.25
  222.5 1.9 fusion.52
  224.5 14.5 %iota_compare_fusion.13 = pred[4096,5120]{1,0:T(32,128)(4,1)} fusion(s32[4096]{0:T(1024)S(1)} %add_select_fusion), kind=kLoop, calls=%fused_computation.2.clone.1.clone.clone.clone.1 | loop fusion | flops 20971520 | bytes 20987904 | tf_op jit(solution)/shard_map/sc,sd->cd/dot_general | solution.py:52
  239.0 100.2 %all-reduce.5.cloned.1.call-done = bf16[8,512,768]{2,1,0:T(8,128)(2,1)} async-done(((bf16[8,512,768]{2,1,0:T(8,128)(2,1)}), bf16[8,512,768]{2,1,0:T(8,128)(2,1)}) %all-reduce.5.cloned.1.call-update) | async-done | bytes 6291472 | tf_op jit(solution)/shard_map/psum | solution.py:86
  339.2 6.9 multiply_reduce_fusion
  346.1 8.2 %multiply_convert_fusion = (bf16[8,512,768]{2,1,0:T(8,128)(2,1)S(1)}, f32[8,512,768]{2,1,0:T(8,128)}) fusion(f32[768]{0:T(1024)S(1)} %copy-done.13, f32[8,512]{1,0:T(8,128)S(1)} %add_rsqrt_fusion, bf16[8,512,768]{2,1,0:T(8,128)(2,1)S(1)} %copy-done.4, bf16[8,512,768]{2,1,0:T(8,128)(2,1)} %get-tuple-element.6), kind=kLoop, calls=%fused_computation.36 | loop fusion | flops 25165824 | bytes 31476736 | tf_op jit(solution)/shard_map/convert_element_type | solution.py:13
  354.3 42.4 %fusion.30 = bf16[5120,768]{1,0:T(8,128)(2,1)S(1)} fusion(bf16[4096,768]{1,0:T(8,128)(2,1)S(1)} %bitcast.106, pred[4096,5120]{1,0:T(32,128)(4,1)} %iota_compare_fusion.13), kind=kOutput, calls=%fused_computation.45 | convolution fusion | flops 32216186880 | bytes 35127296 | tf_op jit(solution)/shard_map/sc,sd->cd/dot_general | solution.py:52
  396.8 93.2 %all_to_all.10 = bf16[128,40,768]{2,1,0:T(8,128)(2,1)} all-to-all(bf16[128,40,768]{2,1,0:T(8,128)(2,1)S(1)} %bitcast.110), channel_id=1, replica_groups=mesh['part'=1,'tp'=4,'ep'=8] {'ep'}, dimensions={0} | all-to-all | bytes 15728640 | tf_op jit(solution)/shard_map/all_to_all | solution.py:53
  490.0 42.1 %fusion.6 = bf16[16,8,40,3072]{3,2,1,0:T(8,128)(2,1)} fusion(bf16[16,768,3072]{2,1,0:T(8,128)(2,1)} %param.36, bf16[8,16,40,768]{3,2,1,0:T(8,128)(2,1)} %bitcast.111), kind=kOutput, calls=%fused_computation.7 | convolution fusion | flops 24159191040 | bytes 114819072 | tf_op jit(solution)/shard_map/gecd,edf->gecf/dot_general | solution.py:55
  532.0 40.7 %convert_bitcast_fusion = bf16[8,16,40,768]{3,2,0,1:T(8,128)(2,1)} fusion(bf16[16,3072,768]{2,1,0:T(8,128)(2,1)} %param.37, bf16[16,8,40,3072]{3,2,1,0:T(8,128)(2,1)} %fusion.6), kind=kOutput, calls=%fused_computation.47 | convolution fusion | flops 24210309120 | bytes 114819072 | tf_op jit(solution)/shard_map/gecf,efd->gecd/dot_general | solution.py:56
  572.7 6.9 copy.26
  579.7 6.4 all-to-all-start.1
  586.1 8.3 %fusion.83 = (f32[4096]{0:T(1024)S(1)}, f32[4096,128]{0,1:T(8,128)S(1)}) fusion(bf16[4096,768]{1,0:T(8,128)(2,1)} %bitcast.107, f32[768,128]{1,0:T(8,128)S(1)} %copy-done.6), kind=kOutput, calls=%fused_computation.95 | convolution fusion | flops 4832358400 | bytes 8798208 | tf_op jit(solution)/shard_map/dot_general | solution.py:34
  594.4 0.3 fusion.55
  594.8 0.6 multiply_reduce_fusion.1
  595.4 78.6 %all-to-all-done.1 = bf16[128,40,768]{2,1,0:T(8,128)(2,1)} async-done(((bf16[128,40,768]{2,1,0:T(8,128)(2,1)}), bf16[128,40,768]{2,1,0:T(8,128)(2,1)}, u32[]{:S(2)}, u32[]{:S(2)}) %all-to-all-start.1) | async-done | bytes 7864352 | tf_op jit(solution)/shard_map/all_to_all | solution.py:57
  673.9 41.6 %fusion.24 = bf16[4096,768]{1,0:T(8,128)(2,1)} fusion(f32[8,512,768]{2,1,0:T(8,128)} %get-tuple-element.8, bf16[5120,768]{1,0:T(8,128)(2,1)} %bitcast.33, s32[4096]{0:T(1024)S(1)} %copy-done.11, f32[4096]{0:T(1024)S(1)} %multiply_reduce_fusion.1), kind=kOutput, calls=%fused_computation.33 | convolution fusion | flops 32242663424 | bytes 26771456 | tf_op jit(solution)/shard_map/sc,cd->sd/dot_general | solution.py:58
  (50 shorter events, 0.1 us)
Async XLA Ops:
  6.5 51.0 %copy-start = (bf16[8,256,768]{2,1,0:T(8,128)(2,1)S(1)}, bf16[8,256,768]{2,1,0:T(8,128)(2,1)}, u32[]{:S(2)}) copy-start(bf16[8,256,768]{2,1,0:T(8,128)(2,1)} %param.20) | copy-start | bytes 9437188
  6.6 4.4 copy-start.21
  6.6 4.4 copy-start.14
  6.6 175.6 %all-reduce.3.cloned.1.call-start = ((), (), s32[]{:S(2)}) async-start(), calls=%async_computation.2 | async-start | bytes 12582912 | tf_op jit(solution)/shard_map/psum | solution.py:81
  6.6 4.8 copy-start.3
  11.4 3.6 copy-start.15
  15.0 3.6 copy-start.16
  18.6 3.6 copy-start.5
  28.0 15.1 %copy-start.17 = (bf16[192,768]{1,0:T(8,128)(2,1)S(1)}, bf16[192,768]{1,0:T(8,128)(2,1)}, u32[]{:S(2)}) copy-start(bf16[192,768]{1,0:T(8,128)(2,1)} %param.28) | copy-start | bytes 884740
  56.7 0.7 copy-start.9
  56.7 0.8 copy-start.12
  56.7 1.0 copy-start.18
  56.7 282.4 %all-reduce.5.cloned.1.call-start = ((), (), s32[]{:S(2)}) async-start(), calls=%async_computation.3 | async-start | bytes 12582912 | tf_op jit(solution)/shard_map/psum | solution.py:86
  57.4 167.1 %copy-start.7 = (s32[1,4,8,128]{3,1,2,0:T(4,128)}, s32[1,4,8,128]{3,1,2,0:T(4,128)S(1)}, u32[]{:S(2)}) copy-start(s32[1,4,8,128]{3,1,2,0:T(4,128)S(1)} %copy.32) | copy-start | bytes 49156
  62.8 128.9 %copy-start.19 = (bf16[768,192]{0,1:T(8,128)(2,1)S(1)}, bf16[768,192]{0,1:T(8,128)(2,1)}, u32[]{:S(2)}) copy-start(bf16[768,192]{0,1:T(8,128)(2,1)} %param.30) | copy-start | bytes 884740
  62.8 129.0 %copy-start.22 = (f32[768]{0:T(1024)S(1)}, f32[768]{0:T(1024)}, u32[]{:S(2)}) copy-start(f32[768]{0:T(1024)} %param.29) | copy-start | bytes 9220
  196.8 10.0 %copy-start.20 = (bf16[192,768]{1,0:T(8,128)(2,1)S(1)}, bf16[192,768]{1,0:T(8,128)(2,1)}, u32[]{:S(2)}) copy-start(bf16[192,768]{1,0:T(8,128)(2,1)} %param.33) | copy-start | bytes 884740
  196.9 9.9 %copy-start.23 = (bf16[8,256,192]{1,2,0:T(8,128)(2,1)S(1)}, bf16[8,256,192]{1,2,0:T(8,128)(2,1)}, u32[]{:S(2)}) copy-start(bf16[8,256,192]{1,2,0:T(8,128)(2,1)} %convolution_convert_fusion) | copy-start | bytes 2359300
  224.5 14.5 %copy-start.10 = (s32[4096]{0:T(1024)}, s32[4096]{0:T(1024)S(1)}, u32[]{:S(2)}) copy-start(s32[4096]{0:T(1024)S(1)} %add_select_fusion) | copy-start | bytes 49156
  239.0 107.1 %copy-start.13 = (f32[768]{0:T(1024)S(1)}, f32[768]{0:T(1024)}, u32[]{:S(2)}) copy-start(f32[768]{0:T(1024)} %param.34) | copy-start | bytes 9220
  339.2 6.9 copy-start.4
  354.3 42.5 %copy-start.2 = (bf16[8,512,768]{2,1,0:T(8,128)(2,1)}, bf16[8,512,768]{2,1,0:T(8,128)(2,1)S(1)}, u32[]{:S(2)}) copy-start(bf16[8,512,768]{2,1,0:T(8,128)(2,1)S(1)} %get-tuple-element.7) | copy-start | bytes 18874372
  579.6 6.4 copy-start.6
  579.7 94.3 %all-to-all-start.1 = ((bf16[128,40,768]{2,1,0:T(8,128)(2,1)}), bf16[128,40,768]{2,1,0:T(8,128)(2,1)}, u32[]{:S(2)}, u32[]{:S(2)}) async-start(bf16[128,40,768]{2,1,0:T(8,128)(2,1)} %bitcast.108), calls=%async_computation.1 | async-start | bytes 15728640 | tf_op jit(solution)/shard_map/all_to_all | solution.py:57
  586.1 8.7 %copy-start.8 = (s32[1,4,8,128]{3,1,2,0:T(4,128)S(1)}, s32[1,4,8,128]{3,1,2,0:T(4,128)}, u32[]{:S(2)}) copy-start(s32[1,4,8,128]{3,1,2,0:T(4,128)} %copy-done.7) | copy-start | bytes 49156
  586.1 87.8 %copy-start.11 = (s32[4096]{0:T(1024)S(1)}, s32[4096]{0:T(1024)}, u32[]{:S(2)}) copy-start(s32[4096]{0:T(1024)} %copy-done.10) | copy-start | bytes 49156
  673.9 41.6 %copy-start.1 = (bf16[8,256,768]{2,1,0:T(8,128)(2,1)S(1)}, bf16[8,256,768]{2,1,0:T(8,128)(2,1)}, u32[]{:S(2)}) copy-start(bf16[8,256,768]{2,1,0:T(8,128)(2,1)} %param.20) | copy-start | bytes 9437188
Sparse Core Ops, SparseCore 0:
  56.9 125.2 all-reduce.2
  217.6 121.4 all-reduce.4
where the time goes:
time: 731 us; the launch traced here: 723 us
  waiting for transfers between devices  298 us (41%)
  matrix products  245 us (34%)
  blocking collectives  93.2 us (13%)
  other arithmetic  50.7 us (7%)
  local copies, waits for them, and re-layouts  14.4 us (2%)
  between operations  14.2 us (2%)
    psum x2, waiting for transfers between devices, layer(): attn_sum = lax.psum(partial.astype(jnp.bfloat16), 'tp')  220 us
    all_to_all x1, blocking collectives, expert_layer(): lax.all_to_all(send_buf.reshape(experts, capacity, d_model), 'ep', 0, 0,...  93.2 us
    all_to_all x1, waiting for transfers between devices, expert_layer(): lax.all_to_all(expert_out.reshape(experts, capacity, d_model), 'ep', 0, 0...  78.6 us
    dot_general x1, matrix products, expert_layer(): jnp.einsum('sc,sd->cd', dispatch, normed, preferred_element_type=jnp.floa...  42.4 us
    dot_general x1, matrix products, expert_layer(): jnp.einsum('gecd,edf->gecf', received, w_in, preferred_element_type=jnp.f...  42.1 us
    dot_general x1, matrix products, expert_layer(): jnp.einsum('sc,cd->sd', dispatch, returned.reshape(experts * capacity, d_...  41.6 us
    dot_general x1, matrix products, expert_layer(): jnp.einsum('gecf,efd->gecd', hidden, w_out, preferred_element_type=jnp.fl...  40.7 us
    sub x2, matrix products, attention_heads(): weights = jax.nn.softmax(scores, axis=-1).astype(jnp.bfloat16)  25 us
  transfers between devices with their start and end apart: 3, of which 3 were waited for; matrix products, arithmetic and copies ran while one was open for 5% of the time, Pallas kernels for 0%

commit v1 on v0

v1 whole, which is shorter than its diff:
```python
import functools

import jax
import jax.numpy as jnp
from jax import lax
from jax.experimental import pallas as pl
from jax.experimental.pallas import tpu as pltpu
from jax.sharding import PartitionSpec as P

EPSILON = 1e-6
NEG_LARGE = -1e30
MESH = pl.DeviceIdType.MESH
BF16 = jnp.bfloat16
F32 = jnp.float32
LANES = 128
VMEM_LIMIT = 67043328


def rms_norm(upcast, gain_vec):
    mean_sq = jnp.mean(upcast * upcast, axis=-1, keepdims=True)
    return (upcast * lax.rsqrt(mean_sq + EPSILON) * gain_vec).astype(BF16)


def dot(a, b):
    return jnp.dot(a, b, preferred_element_type=F32)


def dot_nt(a, b):
    return lax.dot_general(a, b, (((1,), (1,)), ((), ())), preferred_element_type=F32)


def softmax(scores):
    exps = jnp.exp(scores - jnp.max(scores, axis=-1, keepdims=True))
    return (exps * (1.0 / jnp.sum(exps, axis=-1, keepdims=True))).astype(BF16)


def low_lanes(rows):
    return lax.broadcasted_iota(jnp.int32, (rows, LANES), 1) < LANES // 2


def pack_qkv(w_query, w_key, w_value):
    half, full = LANES // 2, LANES
    blank = jnp.zeros((w_query.shape[0], half), w_query.dtype)
    return jnp.concatenate([w_query, blank, w_key[:, :full], w_value[:, :full], w_key[:, full:], w_value[:, full:]], axis=1)


def pack_out(w_output):
    blank = jnp.zeros((LANES // 2, w_output.shape[1]), w_output.dtype)
    return jnp.concatenate([w_output[:LANES], blank, w_output[LANES:]], axis=0)


def remote(src, dst, send_sem, recv_sem, **device):
    return pltpu.make_async_remote_copy(src_ref=src, dst_ref=dst, send_sem=send_sem, recv_sem=recv_sem, device_id=device, device_id_type=MESH)


def barrier(devices):
    sem = pltpu.get_barrier_semaphore()
    for device in devices:
        pl.semaphore_signal(sem, inc=1, device_id=device, device_id_type=MESH)
    pl.semaphore_wait(sem, len(devices))


def self_kernel(tp, ep, dec_ref, gain_ref, w_ref, bias_ref, wq_ref, wo_ref, ctx_ref, wq_all, wo_all, dec_buf, head_buf, ctx_buf, relay, wq_buf, wo_buf, dec_sem, load_sem, ctx_send, ctx_recv, own_sem, wy_send, wy_recv, wx_send, wx_recv, wd_send, wd_recv):
    t, e = lax.axis_index('tp'), lax.axis_index('ep')
    right, left, across = lax.rem(t + 1, tp), lax.rem(t + tp - 1, tp), lax.rem(t + 2, tp)
    x_right, x_left = lax.rem(e + 2, ep), lax.rem(e + ep - 2, ep)
    core, x = lax.rem(e, 2), e // 2
    x_pos_left, x_pos_right, x_across = x_left // 2, x_right // 2, lax.rem(x + 2, ep // 2)
    partner = e + 1 - 2 * core
    mate = 1 - core
    seqs, length = dec_ref.shape[0], dec_ref.shape[1]
    per = seqs // tp
    heads = bias_ref.shape[0]
    loads = [pltpu.make_async_copy(wq_ref, wq_buf, load_sem.at[0]), pltpu.make_async_copy(wo_ref, wo_buf, load_sem.at[1])]
    for load in loads:
        load.start()

    def seq_at(k):
        off = jnp.where(k < per, 2, jnp.where(k < 2 * per, 1, jnp.where(k < 3 * per, 3, 0)))
        return per * lax.rem(t + off, tp) + lax.rem(k, per)

    def dec_load(k):
        return pltpu.make_async_copy(dec_ref.at[seq_at(k)], dec_buf.at[lax.rem(k, 2)], dec_sem.at[lax.rem(k, 2)])

    dec_load(0).start()
    barrier([{'tp': right}, {'tp': left}, {'ep': x_right}, {'ep': x_left}, {'ep': partner}])
    for load in loads:
        load.wait()
    own_w = [pltpu.make_async_copy(wq_buf, wq_all.at[t], load_sem.at[0]), pltpu.make_async_copy(wo_buf, wo_all.at[t], load_sem.at[1])]
    for load in own_w:
        load.start()
    bufs, alls = (wq_buf, wo_buf), (wq_all, wo_all)

    def wy_own(a, side):
        return remote(bufs[a].at[core, x], alls[a].at[t, core, x], wy_send.at[a, side], wy_recv.at[a, side], tp=(right, left)[side])

    def wy_forward(a):
        src = alls[a].at[(left, right)[a], core, x]
        return remote(src, src, wy_send.at[a, 2], wy_recv.at[a, 2], tp=(right, left)[a])

    def wx_own(a, which, side):
        src = alls[a].at[(left, right, across)[which], core, x]
        return remote(src, src, wx_send.at[a, which, side], wx_recv.at[a, which, side], ep=(x_right, x_left)[side])

    def wx_forward(a, which):
        src = alls[a].at[(left, right, across)[which], core, (x_pos_left, x_pos_right)[a]]
        return remote(src, src, wx_send.at[a, which, 2], wx_recv.at[a, which, 2], ep=(x_right, x_left)[a])

    def wd(a, which):
        src = alls[a].at[(left, right, across)[which], core]
        return remote(src, src, wd_send.at[a, which], wd_recv.at[a, which], ep=partner)

    def y_stage():
        for a in (0, 1):
            for side in (0, 1):
                wy_own(a, side).wait_recv()
            wy_forward(a).start()
        for which in (0, 1):
            for a in (0, 1):
                for side in (0, 1):
                    wx_own(a, which, side).start()

    def across_stage():
        for a in (0, 1):
            wy_forward(a).wait_recv()
            for side in (0, 1):
                wx_own(a, 2, side).start()

    def x_stage(whichs):
        for which in whichs:
            for a in (0, 1):
                for side in (0, 1):
                    wx_own(a, which, side).wait_recv()
                wx_forward(a, which).start()

    def d_stage(whichs):
        for which in whichs:
            for a in (0, 1):
                wx_forward(a, which).wait_recv()
                wd(a, which).start()

    for a in (0, 1):
        for side in (0, 1):
            wy_own(a, side).start()

    def to_side(i, side):
        return remote(ctx_buf.at[per * (1 + side) + i], ctx_ref.at[t, i], ctx_send.at[side, i], ctx_recv.at[side, i], tp=(right, left)[side])

    def to_relay(side):
        return remote(ctx_buf.at[side], relay.at[side], ctx_send.at[2, side], ctx_recv.at[2, side], tp=(right, left)[side])

    def from_relay(side):
        return remote(relay.at[side], ctx_ref.at[(left, right)[side], side], ctx_send.at[3, side], ctx_recv.at[3, side], tp=(right, left)[side])

    def own_ctx(i):
        return pltpu.make_async_copy(ctx_buf.at[3 * per + i], ctx_ref.at[t, i], own_sem.at[i])

    block = length // 2

    def body(k, carry):
        dec_load(k).wait()

        @pl.when(k + 1 < seqs)
        def _():
            dec_load(k + 1).start()

        normed = rms_norm(dec_buf[lax.rem(k, 2)].astype(F32), gain_ref[...])
        low = low_lanes(length)
        pair = dot(normed, w_ref[:, :2 * LANES])
        q01 = pair[:, :LANES]
        head_buf[0] = jnp.where(low, q01, 0.0).astype(BF16)
        head_buf[1] = jnp.where(low, 0.0, q01).astype(BF16)
        head_buf[2] = pair[:, LANES:].astype(BF16)
        rest = dot(normed, w_ref[:, 2 * LANES:])
        for piece in range(3):
            head_buf[3 + piece] = rest[:, piece * LANES:(piece + 1) * LANES].astype(BF16)
        low_half = low_lanes(block)
        for half in (0, 1):
            rows = slice(half * block, (half + 1) * block)
            keys = slice(0, (half + 1) * block)
            row_ids = half * block + lax.broadcasted_iota(jnp.int32, (block, (half + 1) * block), 0)
            col_ids = lax.broadcasted_iota(jnp.int32, (block, (half + 1) * block), 1)
            mixed = []
            for head in range(heads):
                key_at, value_at = (3, 4) if head < 2 else (5, 5)
                scores = dot_nt(head_buf[head, rows], head_buf[key_at, keys]) + bias_ref[head, rows, keys]
                scores = jnp.where(col_ids <= row_ids, scores, NEG_LARGE)
                mixed.append(dot(softmax(scores), head_buf[value_at, keys]))
            ctx_buf[k, rows, :LANES] = jnp.where(low_half, mixed[0], mixed[1]).astype(BF16)
            ctx_buf[k, rows, LANES:] = mixed[2].astype(BF16)

        @pl.when(k == 0)
        def _():
            to_relay(0).start()
            y_stage()

        @pl.when(k == 1)
        def _():
            to_relay(1).start()
            across_stage()

        for side in (0, 1):
            for i in range(per):
                @pl.when(k == per * (1 + side) + i)
                def _(side=side, i=i):
                    to_side(i, side).start()

        @pl.when(k == 2)
        def _():
            to_relay(0).wait_recv()
            from_relay(0).start()

        @pl.when(k == 3)
        def _():
            to_relay(1).wait_recv()
            from_relay(1).start()

        @pl.when(k == 4)
        def _():
            x_stage((0, 1))

        @pl.when(k == 6)
        def _():
            x_stage((2,))
            d_stage((0, 1))

        for i in range(per):
            @pl.when(k == 3 * per + i)
            def _(i=i):
                own_ctx(i).start()

        return carry

    lax.fori_loop(0, seqs, body, 0)
    d_stage((2,))
    for load in own_w:
        load.wait()
    for i in range(per):
        own_ctx(i).wait()
    for side in (0, 1):
        for i in range(per):
            to_side(i, side).wait()
        to_relay(side).wait_send()
        from_relay(side).wait()
    for a in (0, 1):
        for side in (0, 1):
            wy_own(a, side).wait_send()
        wy_forward(a).wait_send()
        for which in range(3):
            for side in (0, 1):
                wx_own(a, which, side).wait_send()
            wx_forward(a, which).wait_send()
            wd(a, which).wait()


def cross_kernel(tp, ep, cap, experts, ctx_ref, w_ref, wo_ref, dec_ref, enc_ref, pad_ref, gain_cross_ref, gain_ffn_ref, router_ref, idx_row_ref, idx_col_ref, y2_ref, send_ref, gate_ref, slot_ref, dec_buf, enc_buf, y1_buf, x_buf, q_buf, kv_buf, acc_buf, y2_buf, route_buf, tri_buf, key_buf, dec_sem, enc_sem, y_send, y_recv, out_sem):
    t = lax.axis_index('tp')
    right, left, across = lax.rem(t + 1, tp), lax.rem(t + tp - 1, tp), lax.rem(t + 2, tp)
    seqs, length, width = y2_buf.shape
    per = seqs // tp
    span = experts // ep
    share = span // tp
    wo_rows = 2 * LANES

    def load(i):
        return (pltpu.make_async_copy(dec_ref.at[per * t + i], dec_buf.at[i], dec_sem.at[i]), pltpu.make_async_copy(enc_ref.at[per * t + i], enc_buf.at[i], enc_sem.at[i]))

    for i in range(per):
        for copy in load(i):
            copy.start()
    barrier([{'tp': right}, {'tp': left}])

    def own(i, side):
        src = y2_buf.at[per * t + i]
        return remote(src, src, y_send.at[side, i], y_recv.at[side, i], tp=(right, left)[side])

    def forward(side):
        src = y2_buf.at[per * (left, right)[side] + side]
        return remote(src, src, y_send.at[2, side], y_recv.at[2, side], tp=(right, left)[side])

    def write(s):
        return pltpu.make_async_copy(y2_buf.at[s], y2_ref.at[s], out_sem.at[s])

    low = low_lanes(length)

    def attend(i, carry):
        for copy in load(i):
            copy.wait()
        total = dec_buf[i].astype(F32)
        for row in range(tp):
            total = total + dot(ctx_ref[row, i], wo_ref[row, :wo_rows])
        y1 = total.astype(BF16)
        y1_buf[...] = y1
        x_buf[...] = rms_norm(y1.astype(F32), gain_cross_ref[...])
        acc_buf[...] = jnp.zeros_like(acc_buf)
        pad_bias = jnp.where(pad_ref[pl.ds(per * t + i, 1), :] == 0, 0.0, NEG_LARGE)

        def per_row(row, inner):
            pair = dot(x_buf[...], w_ref[row, :, :2 * LANES])
            q01 = pair[:, :LANES]
            q_buf[0] = jnp.where(low, q01, 0.0).astype(BF16)
            q_buf[1] = jnp.where(low, 0.0, q01).astype(BF16)
            q_buf[2] = pair[:, LANES:].astype(BF16)
            rest = dot(enc_buf[i], w_ref[row, :, 2 * LANES:])
            for piece in range(3):
                kv_buf[piece] = rest[:, piece * LANES:(piece + 1) * LANES].astype(BF16)
            mixed = []
            for head in range(3):
                key_at, value_at = (0, 1) if head < 2 else (2, 2)
                scores = dot_nt(q_buf[head], kv_buf[key_at]) + pad_bias
                mixed.append(dot(softmax(scores), kv_buf[value_at]))
            c01 = jnp.where(low, mixed[0], mixed[1]).astype(BF16)
            acc_buf[...] += dot(c01, wo_ref[row, wo_rows:wo_rows + LANES]) + dot(mixed[2].astype(BF16), wo_ref[row, wo_rows + LANES:])
            return inner

        lax.fori_loop(0, tp, per_row, 0)
        y2_buf[per * t + i] = (y1_buf[...].astype(F32) + acc_buf[...]).astype(BF16)
        for step in range(per):
            @pl.when(i == step)
            def _(step=step):
                for side in (0, 1):
                    own(step, side).start()
        write(per * t + i).start()
        return carry

    lax.fori_loop(0, per, attend, 0)

    w_full = router_ref[...]
    w_high = w_full.astype(BF16)
    w_rest = w_full - w_high.astype(F32)
    w_mid = w_rest.astype(BF16)
    route_buf[:, :experts] = w_high
    route_buf[:, experts:2 * experts] = w_mid
    route_buf[:, 2 * experts:] = (w_rest - w_mid.astype(F32)).astype(BF16)
    row_ids = lax.broadcasted_iota(jnp.int32, (length, length), 0)
    col_ids = lax.broadcasted_iota(jnp.int32, (length, length), 1)
    tri_buf[0] = jnp.where(col_ids <= row_ids, 1.0, 0.0).astype(BF16)
    tri_buf[1] = jnp.where(row_ids <= col_ids, 1.0, 0.0).astype(BF16)
    lane_e = lax.broadcasted_iota(jnp.int32, (length, experts), 1)
    sub_e = lax.broadcasted_iota(jnp.int32, (experts, length), 0)
    lane_s = lax.broadcasted_iota(jnp.int32, idx_col_ref.shape, 1)
    slot_ref[...] = jnp.zeros_like(slot_ref)
    gate_ref[...] = jnp.zeros_like(gate_ref)

    def choice_col(s):
        return jnp.sum(jnp.where(lane_s == s, idx_col_ref[...], 0), axis=1, keepdims=True)

    def place(s, carry):
        base_row, base_col = carry
        col = choice_col(s)
        hot = jnp.where(lane_e == col, 1.0, 0.0)
        count = dot(tri_buf[0], hot.astype(BF16)) + base_row
        pos = jnp.sum(hot * count, axis=1, keepdims=True) - 1.0
        slot = jnp.where(pos < cap, col * cap + pos.astype(jnp.int32), -1)
        slot_ref[...] += jnp.where(lane_s == s, slot, 0)
        row = idx_row_ref[pl.ds(s, 1), :]
        hot_t = jnp.where(sub_e == row, 1.0, 0.0)
        count_t = dot(hot_t.astype(BF16), tri_buf[1]) + base_col
        pos_t = jnp.sum(hot_t * count_t, axis=0, keepdims=True) - 1.0
        mine = (pos_t < cap) & (lax.rem(row // share, tp) == t)
        key_buf[pl.ds(s, 1), :] = jnp.where(mine, (row // span) * (share * cap) + lax.rem(row, share) * cap + pos_t.astype(jnp.int32), -1)
        return count[length - 1:, :], count_t[:, length - 1:]

    lax.fori_loop(0, seqs, place, (jnp.zeros((1, experts), F32), jnp.zeros((experts, 1), F32)))
    send_ref[...] = jnp.zeros_like(send_ref)
    chunk = share * cap

    def consume(n, carry):
        near = jnp.where(lax.rem(n, 2) == 0, left, right)
        row = jnp.where(n < per, t, jnp.where(n < 3 * per, near, across))
        half = jnp.where(n < per, n, jnp.where(n < 3 * per, lax.rem(n // 2 + 1, 2), lax.rem(n, 2)))
        s = per * row + half

        @pl.when(n == 2)
        def _():
            own(0, 0).wait_recv()
            forward(0).start()

        @pl.when(n == 3)
        def _():
            own(0, 1).wait_recv()

        @pl.when(n == 4)
        def _():
            own(1, 0).wait_recv()
            own(1, 1).wait_recv()
            forward(1).start()

        @pl.when(n == 6)
        def _():
            forward(0).wait_recv()

        @pl.when(n == 7)
        def _():
            forward(1).wait_recv()

        @pl.when(n >= per)
        def _():
            write(s).start()

        normed = rms_norm(y2_buf[s].astype(F32), gain_ffn_ref[...])
        x_buf[...] = normed
        parts = dot(normed, route_buf[...])
        logits = parts[:, :experts] + (parts[:, experts:2 * experts] + parts[:, 2 * experts:])
        exps = jnp.exp(logits - jnp.max(logits, axis=-1, keepdims=True))
        picked = jnp.sum(jnp.where(lane_e == choice_col(s), exps, 0.0), axis=-1, keepdims=True)
        gate_ref[...] += jnp.where(lane_s == s, picked / jnp.sum(exps, axis=-1, keepdims=True), 0.0)
        key = key_buf[pl.ds(s, 1), :]

        def dispatch(d, inner):
            rows = pl.ds(d * chunk, chunk)
            hot = jnp.where(lax.broadcasted_iota(jnp.int32, (chunk, length), 0) + d * chunk == key, 1.0, 0.0).astype(BF16)
            send_ref[rows, :] = (send_ref[rows, :].astype(F32) + dot(hot, x_buf[...])).astype(BF16)
            return inner

        lax.fori_loop(0, ep, dispatch, 0)
        return carry

    lax.fori_loop(0, seqs, consume, 0)
    for s in range(seqs):
        write(s).wait()
    for side in (0, 1):
        for i in range(per):
            own(i, side).wait_send()
        forward(side).wait_send()


def expert_kernel(tp, ep, cap, send_ref, w_in_ref, w_out_ref, y2_ref, gate_ref, slot_ref, out_ref, got, staged, out_stage, out_buf, all_buf, acc_buf, y2_buf, w_in_buf, w_out_buf, xd_send, xd_recv, xr_send, xr_recv, y_send, y_recv, w_sem, own_sem, y2_sem, out_sem):
    t, e = lax.axis_index('tp'), lax.axis_index('ep')
    right, left, across = lax.rem(t + 1, tp), lax.rem(t + tp - 1, tp), lax.rem(t + 2, tp)
    seqs, length, width = y2_buf.shape
    share = staged.shape[0]
    pairs = got.shape[1]
    in_pair = share // pairs
    rows2 = in_pair * cap
    ff = w_in_buf.shape[2]
    barrier([{'tp': right}, {'tp': left}] + [{'ep': lax.rem(e + o, ep)} for o in range(1, ep)])

    def dispatch(o, p):
        return remote(send_ref.at[lax.rem(e + o, ep), p], got.at[e, p], xd_send.at[o, p], xd_recv.at[o, p], ep=lax.rem(e + o, ep))

    def give_back(o, p):
        return remote(out_buf.at[p, lax.rem(e + o, ep)], all_buf.at[t, p, e], xr_send.at[o, p], xr_recv.at[o, p], ep=lax.rem(e + o, ep))

    def dispatch_in(o, p):
        return remote(send_ref.at[0, p], got.at[lax.rem(e + ep - o, ep), p], xd_send.at[o, p], xd_recv.at[o, p], ep=lax.rem(e + o, ep))

    def give_in(o, p):
        return remote(out_buf.at[p, 0], all_buf.at[t, p, lax.rem(e + ep - o, ep)], xr_send.at[o, p], xr_recv.at[o, p], ep=lax.rem(e + o, ep))

    def own_dispatch(p):
        return pltpu.make_async_copy(send_ref.at[e, p], got.at[e, p], own_sem.at[p])

    def weights(j):
        return (pltpu.make_async_copy(w_in_ref.at[share * t + j], w_in_buf.at[j % 2], w_sem.at[0, j % 2]), pltpu.make_async_copy(w_out_ref.at[share * t + j], w_out_buf.at[j % 2], w_sem.at[1, j % 2]))

    order = (4, 2, 6, 3, 5, 1, 7)
    for p in range(pairs):
        for o in order:
            dispatch(o, p).start()
        own_dispatch(p).start()
    for j in (0, 1):
        for copy in weights(j):
            copy.start()
    y2_load = pltpu.make_async_copy(y2_ref, y2_buf, y2_sem)
    y2_load.start()
    acc_buf[...] = jnp.zeros_like(acc_buf)

    def share_out(p, side):
        src = all_buf.at[t, p]
        return remote(src, src, y_send.at[side, p], y_recv.at[side, p], tp=(right, left)[side])

    def pass_on(p, side):
        src = all_buf.at[(left, right)[side], p, pl.ds(side * (ep // 2), ep // 2)]
        return remote(src, src, y_send.at[2 + side, p], y_recv.at[2 + side, p], tp=(right, left)[side])

    def came(row, p, side):
        dst = all_buf.at[row, p]
        return remote(dst, dst, y_send.at[side, p], y_recv.at[side, p], tp=right)

    def came_on(p, side):
        dst = all_buf.at[across, p, pl.ds(side * (ep // 2), ep // 2)]
        return remote(dst, dst, y_send.at[2 + side, p], y_recv.at[2 + side, p], tp=right)

    lane_s = lax.broadcasted_iota(jnp.int32, slot_ref.shape, 1)

    def mix(row, p):
        def chunk(s, carry):
            slot = jnp.sum(jnp.where(lane_s == s, slot_ref[...], 0), axis=1, keepdims=True)
            hit = (slot >= 0) & (lax.rem(slot // rows2, tp * pairs) == row * pairs + p)
            key = jnp.where(hit, (slot // (rows2 * pairs * tp)) * rows2 + lax.rem(slot, rows2), -1)
            hot = jnp.where(lax.broadcasted_iota(jnp.int32, (length, ep * rows2), 1) == key, 1.0, 0.0).astype(BF16)
            acc_buf[s] = (acc_buf[s].astype(F32) + dot(hot, all_buf[row, p].reshape(ep * rows2, width))).astype(BF16)
            return carry

        lax.fori_loop(0, seqs, chunk, 0)

    for p in range(pairs):
        own_dispatch(p).wait()
        for o in range(1, ep):
            dispatch_in(o, p).wait_recv()

        def unpack(g, carry):
            block = got[g, p].astype(F32)
            for jj in range(in_pair):
                staged[p * in_pair + jj, pl.ds(pl.multiple_of(g * cap, 8), cap), :] = block[jj * cap:(jj + 1) * cap]
            return carry

        lax.fori_loop(0, ep, unpack, 0)
        for jj in range(in_pair):
            j = p * in_pair + jj
            for copy in weights(j):
                copy.wait()
            inputs = staged[j].astype(BF16)
            staged[j] = jnp.zeros_like(staged[j])

            def ffn(c, carry):
                cols = pl.ds(pl.multiple_of(c * width, LANES), width)
                hidden = jnp.maximum(dot(inputs, w_in_buf[j % 2, :, cols]), 0.0).astype(BF16)
                staged[j] += dot(hidden, w_out_buf[j % 2, cols, :])
                return carry

            lax.fori_loop(0, ff // width, ffn, 0)
            if j + 2 < share:
                for copy in weights(j + 2):
                    copy.start()

        def repack(g, carry):
            for jj in range(in_pair):
                out_stage[pl.ds(jj * cap, cap), :] = staged[p * in_pair + jj, pl.ds(pl.multiple_of(g * cap, 8), cap), :]
            out_buf[p, g] = out_stage[...].astype(BF16)
            return carry

        lax.fori_loop(0, ep, repack, 0)
        for o in order:
            give_back(o, p).start()
        all_buf[t, p, e] = out_buf[p, e]

    for p in range(pairs):
        for o in range(1, ep):
            give_in(o, p).wait_recv()
        for side in (0, 1):
            share_out(p, side).start()
        if p == 0:
            mix(t, p)
    mix(t, 1)
    for p in range(pairs):
        came(left, p, 0).wait_recv()
        pass_on(p, 0).start()
        came(right, p, 1).wait_recv()
        pass_on(p, 1).start()
        mix(left, p)
        mix(right, p)
    y2_load.wait()
    came_on(0, 0).wait_recv()
    came_on(0, 1).wait_recv()
    mix(across, 0)
    came_on(1, 0).wait_recv()
    came_on(1, 1).wait_recv()
    mix(across, 1)

    def write(s):
        return pltpu.make_async_copy(y2_buf.at[s], out_ref.at[s], out_sem.at[s])

    def finish(s, carry):
        gate = jnp.sum(jnp.where(lane_s == s, gate_ref[...], 0.0), axis=1, keepdims=True)
        y2_buf[s] = (y2_buf[s].astype(F32) + gate * acc_buf[s].astype(F32)).astype(BF16)
        write(s).start()
        return carry

    lax.fori_loop(0, seqs, finish, 0)
    for s in range(seqs):
        write(s).wait()
    for p in range(pairs):
        for o in range(1, ep):
            dispatch(o, p).wait_send()
            give_back(o, p).wait_send()
        for side in (0, 1):
            share_out(p, side).wait_send()
            pass_on(p, side).wait_send()


def any_spec():
    return pl.BlockSpec(memory_space=pl.ANY)


def vmem_spec():
    return pl.BlockSpec(memory_space=pltpu.VMEM)


def params(number):
    return pltpu.CompilerParams(collective_id=number, has_side_effects=True, vmem_limit_bytes=VMEM_LIMIT)


def solution(mesh):
    tp, ep = mesh.shape['tp'], mesh.shape['ep']
    dma = pltpu.SemaphoreType.DMA
    token_spec = P(('part', 'ep'), None, None)
    row_spec = P(('part', 'ep'), None)
    col_spec = P(None, 'tp')
    head_rows = P('tp', None)
    vec_spec = P(None)
    expert_spec = P('ep', None, None)
    in_specs = (token_spec, token_spec, row_spec, row_spec, P('tp', None, None), vec_spec, col_spec, col_spec, col_spec, head_rows, vec_spec, col_spec, col_spec, col_spec, head_rows, vec_spec, P(None, None), expert_spec, expert_spec)

    def layer(dec_states, enc_states, enc_pad, expert_idx, self_bias, gain_self, wq_self, wk_self, wv_self, wo_self, gain_cross, wq_cross, wk_cross, wv_cross, wo_cross, gain_ffn, w_router, w_in, w_out):
        seqs, length, width = dec_states.shape
        enc_len = enc_states.shape[1]
        per = seqs // tp
        experts = w_router.shape[1]
        tokens = seqs * length
        cap = (5 * tokens + 4 * experts - 1) // (4 * experts)
        share = experts // ep // tp
        heads = self_bias.shape[0]
        w_self = pack_qkv(wq_self, wk_self, wv_self)
        packed = w_self.shape[1]
        chips = ep // 2
        w_cross = pack_qkv(wq_cross, wk_cross, wv_cross).reshape(2, chips, width // ep, packed)
        wo_both = jnp.concatenate([pack_out(wo_self), pack_out(wo_cross)], axis=0)
        wo_len = wo_both.shape[0]
        wo_both = wo_both.reshape(2, chips, wo_len // ep, width)
        ctx, wq_all, wo_all = pl.pallas_call(
            functools.partial(self_kernel, tp, ep),
            name='self_attend',
            out_shape=(
                jax.ShapeDtypeStruct((tp, per, length, 2 * LANES), BF16),
                jax.ShapeDtypeStruct((tp, *w_cross.shape), BF16),
                jax.ShapeDtypeStruct((tp, *wo_both.shape), BF16),
            ),
            in_specs=[any_spec(), vmem_spec(), vmem_spec(), vmem_spec(), any_spec(), any_spec()],
            out_specs=(any_spec(), any_spec(), any_spec()),
            scratch_shapes=[
                pltpu.VMEM((2, length, width), BF16),
                pltpu.VMEM((6, length, LANES), BF16),
                pltpu.VMEM((seqs, length, 2 * LANES), BF16),
                pltpu.VMEM((2, length, 2 * LANES), BF16),
                pltpu.VMEM(w_cross.shape, BF16),
                pltpu.VMEM(wo_both.shape, BF16),
                dma((2,)), dma((2,)), dma((4, 2)), dma((4, 2)), dma((per,)),
                dma((2, 3)), dma((2, 3)), dma((2, 3, 3)), dma((2, 3, 3)), dma((2, 3)), dma((2, 3)),
            ],
            compiler_params=params(0),
        )(dec_states, gain_self.reshape(1, width), w_self, self_bias, w_cross, wo_both)
        w_all = wq_all.reshape(tp, width, packed)
        wo_all = wo_all.reshape(tp, wo_len, width)
        y2, send, gate, slot = pl.pallas_call(
            functools.partial(cross_kernel, tp, ep, cap, experts),
            name='cross_attend',
            out_shape=(
                jax.ShapeDtypeStruct((seqs, length, width), BF16),
                jax.ShapeDtypeStruct((ep * share * cap, width), BF16),
                jax.ShapeDtypeStruct((length, seqs), F32),
                jax.ShapeDtypeStruct((length, seqs), jnp.int32),
            ),
            in_specs=[vmem_spec(), vmem_spec(), vmem_spec(), any_spec(), any_spec()] + [vmem_spec()] * 6,
            out_specs=(any_spec(), vmem_spec(), vmem_spec(), vmem_spec()),
            scratch_shapes=[
                pltpu.VMEM((per, length, width), BF16),
                pltpu.VMEM((per, enc_len, width), BF16),
                pltpu.VMEM((length, width), BF16),
                pltpu.VMEM((length, width), BF16),
                pltpu.VMEM((3, length, LANES), BF16),
                pltpu.VMEM((3, enc_len, LANES), BF16),
                pltpu.VMEM((length, width), F32),
                pltpu.VMEM((seqs, length, width), BF16),
                pltpu.VMEM((width, 3 * experts), BF16),
                pltpu.VMEM((2, length, length), BF16),
                pltpu.VMEM((seqs, length), jnp.int32),
                dma((per,)), dma((per,)), dma((3, 2)), dma((3, 2)), dma((seqs,)),
            ],
            compiler_params=params(1),
        )(ctx, w_all, wo_all, dec_states, enc_states, enc_pad, gain_cross.reshape(1, width), gain_ffn.reshape(1, width), w_router, expert_idx, expert_idx.T)
        pairs = 2
        rows2 = share // pairs * cap
        return pl.pallas_call(
            functools.partial(expert_kernel, tp, ep, cap),
            name='experts',
            out_shape=jax.ShapeDtypeStruct((seqs, length, width), BF16),
            in_specs=[any_spec(), any_spec(), any_spec(), any_spec(), vmem_spec(), vmem_spec()],
            out_specs=any_spec(),
            scratch_shapes=[
                pltpu.VMEM((ep, pairs, rows2, width), BF16),
                pltpu.VMEM((share, ep * cap, width), F32),
                pltpu.VMEM((rows2, width), F32),
                pltpu.VMEM((pairs, ep, rows2, width), BF16),
                pltpu.VMEM((tp, pairs, ep, rows2, width), BF16),
                pltpu.VMEM((seqs, length, width), BF16),
                pltpu.VMEM((seqs, length, width), BF16),
                pltpu.VMEM((2, width, w_in.shape[2]), BF16),
                pltpu.VMEM((2, w_in.shape[2], width), BF16),
                dma((ep, pairs)), dma((ep, pairs)), dma((ep, pairs)), dma((ep, pairs)),
                dma((4, pairs)), dma((4, pairs)), dma((2, 2)), dma((pairs,)), dma, dma((seqs,)),
            ],
            compiler_params=params(2),
        )(send.reshape(ep, pairs, rows2, width), w_in, w_out, y2, gate, slot)

    return jax.shard_map(layer, mesh=mesh, in_specs=in_specs, out_specs=token_spec, check_vma=False)
```

time: 731 us -> 275 us (0.38)
  waiting for transfers between devices: 298 us -> 0 us
  Pallas kernels: 0 us -> 249 us
  matrix products: 245 us -> 0 us
  blocking collectives: 93.2 us -> 0 us
  other arithmetic: 50.7 us -> 0 us
  between operations: 14.2 us -> 0.18 us
  local copies, waits for them, and re-layouts: 14.4 us -> 22.9 us
    pallas_call x0 -> x3, Pallas kernels: none -> 249 us  [the longest x1 125 us: layer(): pl.pallas_call(functools.partial(expert_kernel, tp, ep, cap), name='exper...]
    dot_general x13 -> x0, matrix products: 220 us -> none  [the longest x1 42.4 us: expert_layer(): jnp.einsum('sc,sd->cd', dispatch, normed, preferred_element_type=jnp.floa...]
    psum x2 -> x0, waiting for transfers between devices: 220 us -> none  [layer(): attn_sum = lax.psum(partial.astype(jnp.bfloat16), 'tp')]
    all_to_all x1 -> x0, blocking collectives: 93.2 us -> none  [expert_layer(): lax.all_to_all(send_buf.reshape(experts, capacity, d_model), 'ep', 0, 0,...]
    all_to_all x1 -> x0, waiting for transfers between devices: 78.6 us -> none  [expert_layer(): lax.all_to_all(expert_out.reshape(experts, capacity, d_model), 'ep', 0, 0...]
    sub x2 -> x0, matrix products: 25 us -> none  [attention_heads(): weights = jax.nn.softmax(scores, axis=-1).astype(jnp.bfloat16)]
    reduce_sum x6 -> x0, other arithmetic: 23.5 us -> none  [the longest x3 20.6 us: rms_norm(): mean_sq = jnp.mean(upcast * upcast, axis=-1, keepdims=True)]
    dot_general x1 -> x0, other arithmetic: 14.5 us -> none  [expert_layer(): jnp.einsum('sc,sd->cd', dispatch, normed, preferred_element_type=jnp.floa...]
  transfers between devices with their start and end apart: 3 -> 0, of which waited for: 3 -> 0; matrix products, arithmetic and copies ran while one was open for 5% -> 0% of each run, Pallas kernels for 0% -> 0%
where the time goes in v1:
time: 275 us; the launch traced here: 272 us
  Pallas kernels  249 us (91%)
  local copies, waits for them, and re-layouts  22.9 us (8%)
    pallas_call x1, Pallas kernels, layer(): pl.pallas_call(functools.partial(expert_kernel, tp, ep, cap), name='exper...  125 us
    pallas_call x1, Pallas kernels, layer(): pl.pallas_call(functools.partial(cross_kernel, tp, ep, cap, experts), nam...  74.8 us
    pallas_call x1, Pallas kernels, layer(): pl.pallas_call(functools.partial(self_kernel, tp, ep), name='self_attend'...  48.7 us
    unnamed x27, local copies, waits for them, and re-layouts  12.1 us

profile of v1, /device:TPU:97, one launch (start us, length us, event | category | flops | bytes accessed | tf_op | source)
XLA Modules:
  0.0 272.0 jit_solution(11106919371537735535)
XLA Ops:
  0.0 0.0 copy-start.1
  0.0 0.0 copy-start.3
  0.0 0.0 copy-start.2
  0.0 0.0 copy-start.4
  0.0 1.4 reshape.24.gain_ref
  1.4 1.3 reshape.29.gain_cross_ref
  2.7 1.3 reshape.30.gain_ffn_ref
  3.9 0.9 slice.38
  4.8 0.2 copy.30
  5.0 0.9 slice.39
  5.9 0.2 copy.31
  6.1 0.9 slice.36
  7.0 0.2 copy.28
  7.2 0.9 slice.37
  8.1 0.2 copy.29
  8.3 1.6 copy.27
  9.9 1.1 copy.24
  11.0 1.8 concatenate.9.w_ref
  12.8 0.9 slice_dynamic-update-slice_fusion.1
  13.8 0.9 slice_dynamic-update-slice_fusion.5
  14.7 0.0 copy-done.1
  14.8 0.0 copy-start
  14.8 0.9 copy-done
  15.7 0.0 copy-done.4
  15.7 0.0 copy-done.2
  15.7 0.0 copy-done.3
  15.8 1.3 copy.26
  17.1 48.7 %self_attend.1 = (bf16[4,2,512,256]{3,2,1,0:T(8,128)(2,1)}, bf16[4,2,4,96,640]{4,3,2,1,0:T(8,128)(2,1)}, bf16[4,2,4,64,768]{4,3,2,1,0:T(8,128)(2,1)}) custom-call(bf16[8,512,768]{2,1,0:T(8,128)(2,1)} %dec_ref.3, f32[1,768]{1,0:T(1,128)} %reshape.24.gain_ref, bf16[768,640]{1,0:T(8,128)(2,1)} %concatenate.9.w_ref, f32[3,512,512]{2,1,0:T(8,128)} %bias_ref.1, ...), custom_call_target="tpu_custom_call" | custom-call | tf_op jit(solution)/shard_map/self_attend/pallas_call | solution.py:622
  65.9 74.8 %cross_attend.1 = (bf16[8,512,768]{2,1,0:T(8,128)(2,1)}, bf16[1280,768]{1,0:T(8,128)(2,1)}, f32[512,8]{1,0:T(8,128)}, s32[512,8]{1,0:T(8,128)}) custom-call(bf16[4,2,512,256]{3,2,1,0:T(8,128)(2,1)} %get-tuple-element.12.ctx_ref, bf16[4,768,640]{2,1,0:T(8,128)(2,1)} %bitcast.6, bf16[4,512,768]{2,1,0:T(8,128)(2,1)} %bitcast.8, bf16[8,512,768]{2,1,0:T(8,128)(2,1)} %dec_ref.3, ...), custom_call_target="tpu_custom_call" | custom-call | tf_op jit(solution)/shard_map/cross_attend/pallas_call | solution.py:646
  140.6 125.4 %experts.1 = bf16[8,512,768]{2,1,0:T(8,128)(2,1)} custom-call(bf16[8,2,80,768]{3,2,1,0:T(8,128)(2,1)} %bitcast.9, bf16[16,768,3072]{2,1,0:T(8,128)(2,1)} %w_in_ref.1, bf16[16,3072,768]{2,1,0:T(8,128)(2,1)} %w_out_ref.1, bf16[8,512,768]{2,1,0:T(8,128)(2,1)} %get-tuple-element.16.y2_ref, f32[512,8]{1,0:T(8,128)} %get-tuple-element.17.gate_ref, ...), custom_call_target="tpu_custom_call" | custom-call | tf_op jit(solution)/shard_map/experts/pallas_call | solution.py:675
  266.1 5.9 %copy.43 = bf16[8,512,768]{2,1,0:T(8,128)(2,1)} copy(bf16[8,512,768]{2,1,0:T(8,128)(2,1)} %experts.1) | data formatting | bytes 12582912
  (11 shorter events, 0.1 us)
Async XLA Ops:
  0.0 14.7 %copy-start.1 = (bf16[192,768]{1,0:T(8,128)(2,1)S(1)}, bf16[192,768]{1,0:T(8,128)(2,1)}, u32[]{:S(2)}) copy-start(bf16[192,768]{1,0:T(8,128)(2,1)} %param.33) | copy-start | bytes 884740
  0.0 15.7 %copy-start.3 = (bf16[768,192]{0,1:T(8,128)(2,1)S(1)}, bf16[768,192]{0,1:T(8,128)(2,1)}, u32[]{:S(2)}) copy-start(bf16[768,192]{0,1:T(8,128)(2,1)} %param.32) | copy-start | bytes 884740
  0.0 15.7 %copy-start.2 = (bf16[768,192]{0,1:T(8,128)(2,1)S(1)}, bf16[768,192]{0,1:T(8,128)(2,1)}, u32[]{:S(2)}) copy-start(bf16[768,192]{0,1:T(8,128)(2,1)} %param.31) | copy-start | bytes 884740
  0.0 15.7 %copy-start.4 = (bf16[768,192]{0,1:T(8,128)(2,1)S(1)}, bf16[768,192]{0,1:T(8,128)(2,1)}, u32[]{:S(2)}) copy-start(bf16[768,192]{0,1:T(8,128)(2,1)} %param.30) | copy-start | bytes 884740
  14.8 0.9 copy-start

commit v2 on v0

v2 whole, which is shorter than its diff:
```python
import functools

import jax
import jax.numpy as jnp
from jax import lax
from jax.experimental import pallas as pl
from jax.experimental.pallas import tpu as pltpu
from jax.sharding import PartitionSpec as P

EPSILON = 1e-6
NEG_LARGE = -1e30
MESH = pl.DeviceIdType.MESH
BF16 = jnp.bfloat16
F32 = jnp.float32
LANES = 128
WIDE = 256
VMEM_LIMIT = 67043328
SIDES = range(2)
ROW = {'axis': -1, 'keepdims': True}
ALL = Ellipsis


def rms_norm(upcast, gain_vec):
    mean_sq = jnp.mean(upcast * upcast, **ROW)
    return (upcast * lax.rsqrt(mean_sq + EPSILON) * gain_vec).astype(BF16)


def dot(a, b):
    return jnp.dot(a, b, preferred_element_type=F32)


def dot_nt(a, b):
    return lax.dot_general(a, b, (((1,), (1,)), ((), ())), preferred_element_type=F32)


def softmax(scores):
    exps = jnp.exp(scores - jnp.max(scores, **ROW))
    return (exps * (1.0 / jnp.sum(exps, **ROW))).astype(BF16)


def low_lanes(rows):
    return lax.broadcasted_iota(jnp.int32, (rows, LANES), 1) < LANES // 2


def pack_qkv(w_query, w_key, w_value, packed):
    half, full = LANES // 2, LANES
    packed[:full + half] = w_query[ALL]
    packed[full + half:2 * full] = jnp.zeros((half, packed.shape[1]), BF16)
    packed[2 * full:3 * full] = w_key[:full]
    packed[3 * full:4 * full] = w_value[:full]
    packed[4 * full:4 * full + half] = w_key[full:]
    packed[4 * full + half:] = w_value[full:]


def remote(src, dst, send_sem, recv_sem, **device):
    return pltpu.make_async_remote_copy(src_ref=src, dst_ref=dst, send_sem=send_sem, recv_sem=recv_sem, device_id=device, device_id_type=MESH)


def greet(devices):
    for device in devices:
        pl.semaphore_signal(pltpu.get_barrier_semaphore(), inc=1, device_id=device, device_id_type=MESH)


def meet(devices):
    pl.semaphore_wait(pltpu.get_barrier_semaphore(), len(devices))


def self_part(tp, ep, dec_ref, gain_ref, bias_ref, wq_self, wk_self, wv_self, wo_self, wq_cross, wk_cross, wv_cross, wo_cross, ctx_ref, wq_all, wo_all, dec_buf, head_buf, ctx_buf, relay, w_ref, dec_sem, ctx_send, ctx_recv, wy_send, wy_recv, wx_send, wx_recv, wd_send, wd_recv):
    t, e = lax.axis_index('tp'), lax.axis_index('ep')
    right, left, across = lax.rem(t + 1, tp), lax.rem(t + tp - 1, tp), lax.rem(t + 2, tp)
    x_right, x_left = lax.rem(e + 2, ep), lax.rem(e + ep - 2, ep)
    chips = ep // 2
    core, x = lax.rem(e, 2), e // 2
    piece = core * chips + x
    piece_left, piece_right = core * chips + x_left // 2, core * chips + x_right // 2
    partner = e + 1 - 2 * core
    seqs, length = dec_ref.shape[0], dec_ref.shape[1]
    per = seqs // tp
    heads = bias_ref.shape[0]
    def seq_at(k):
        off = jnp.where(k < per, 2, jnp.where(k < 2 * per, 1, jnp.where(k < 3 * per, 3, 0)))
        return per * lax.rem(t + off, tp) + lax.rem(k, per)

    def dec_load(k):
        return pltpu.make_async_copy(dec_ref.at[seq_at(k)], dec_buf.at[lax.rem(k, 2)], dec_sem.at[lax.rem(k, 2)])

    dec_load(0).start()
    friends = [{'tp': right}, {'tp': left}, {'tp': across}, {'ep': x_right}, {'ep': x_left}, {'ep': partner}]
    greet(friends)
    pack_qkv(wq_cross, wk_cross, wv_cross, wq_all.at[t])
    wo_all[t, :wo_self.shape[0]] = wo_self[ALL]
    wo_all[t, wo_self.shape[0]:] = wo_cross[ALL]
    meet(friends)
    alls = (wq_all, wo_all)
    rows_of = tuple(buf.shape[1] // ep for buf in alls)

    def rows(a, at):
        return pl.ds(pl.multiple_of(at * rows_of[a], rows_of[a]), rows_of[a])

    def wy_own(a, side):
        src = alls[a].at[t, rows(a, piece)]
        return remote(src, src, wy_send.at[a, side], wy_recv.at[a, side], tp=(right, left)[side])

    def wy_forward(a):
        src = alls[a].at[(left, right)[a], rows(a, piece)]
        return remote(src, src, wy_send.at[a, 2], wy_recv.at[a, 2], tp=(right, left)[a])

    def wx_own(a, which, side):
        src = alls[a].at[(left, right, across)[which], rows(a, piece)]
        return remote(src, src, wx_send.at[a, which, side], wx_recv.at[a, which, side], ep=(x_right, x_left)[side])

    def wx_forward(a, which):
        src = alls[a].at[(left, right, across)[which], rows(a, (piece_left, piece_right)[a])]
        return remote(src, src, wx_send.at[a, which, 2], wx_recv.at[a, which, 2], ep=(x_right, x_left)[a])

    def wd(a, which):
        block_rows = chips * rows_of[a]
        src = alls[a].at[(left, right, across)[which], pl.ds(pl.multiple_of(core * block_rows, block_rows), block_rows)]
        return remote(src, src, wd_send.at[a, which], wd_recv.at[a, which], ep=partner)

    def y_stage():
        for a in SIDES:
            for side in SIDES:
                wy_own(a, side).wait_recv()
            wy_forward(a).start()
        for which in SIDES:
            for a in SIDES:
                for side in SIDES:
                    wx_own(a, which, side).start()

    def across_stage():
        for a in SIDES:
            wy_forward(a).wait_recv()
            for side in SIDES:
                wx_own(a, 2, side).start()

    def x_stage(whichs):
        for which in whichs:
            for a in SIDES:
                for side in SIDES:
                    wx_own(a, which, side).wait_recv()
                wx_forward(a, which).start()

    def d_stage(whichs):
        for which in whichs:
            for a in SIDES:
                wx_forward(a, which).wait_recv()
                wd(a, which).start()

    for a in SIDES:
        for side in SIDES:
            wy_own(a, side).start()
    pack_qkv(wq_self, wk_self, wv_self, w_ref)

    def to_side(i, side):
        return remote(ctx_buf.at[per * (1 + side) + i], ctx_ref.at[t, i], ctx_send.at[side, i], ctx_recv.at[side, i], tp=(right, left)[side])

    def to_relay(side):
        return remote(ctx_buf.at[side], relay.at[side], ctx_send.at[2, side], ctx_recv.at[2, side], tp=(right, left)[side])

    def from_relay(side):
        return remote(relay.at[side], ctx_ref.at[(left, right)[side], side], ctx_send.at[3, side], ctx_recv.at[3, side], tp=(right, left)[side])

    block = length // 2

    def body(k, carry):
        dec_load(k).wait()

        @pl.when(k + 1 < seqs)
        def _():
            dec_load(k + 1).start()

        normed = rms_norm(dec_buf[lax.rem(k, 2)].astype(F32), gain_ref[ALL])
        low = low_lanes(length)
        pair = dot_nt(normed, w_ref[:WIDE])
        q01 = pair[:, :LANES]
        head_buf[0] = jnp.where(low, q01, 0.0).astype(BF16)
        head_buf[1] = jnp.where(low, 0.0, q01).astype(BF16)
        head_buf[2] = pair[:, LANES:].astype(BF16)
        rest = dot_nt(normed, w_ref[WIDE:])
        for piece in range(3):
            head_buf[3 + piece] = rest[:, piece * LANES:(piece + 1) * LANES].astype(BF16)
        low_half = low_lanes(block)
        for half in SIDES:
            span = slice(half * block, (half + 1) * block)
            keys = slice(0, (half + 1) * block)
            row_ids = half * block + lax.broadcasted_iota(jnp.int32, (block, (half + 1) * block), 0)
            col_ids = lax.broadcasted_iota(jnp.int32, (block, (half + 1) * block), 1)
            mixed = []
            for head in range(heads):
                key_at, value_at = (3, 4) if head < 2 else (5, 5)
                scores = dot_nt(head_buf[head, span], head_buf[key_at, keys]) + bias_ref[head, span, keys]
                scores = jnp.where(col_ids <= row_ids, scores, NEG_LARGE)
                mixed.append(dot(softmax(scores), head_buf[value_at, keys]))
            ctx_buf[k, span, :LANES] = jnp.where(low_half, mixed[0], mixed[1]).astype(BF16)
            ctx_buf[k, span, LANES:] = jnp.where(low_half, 0.0, mixed[2]).astype(BF16)

        @pl.when(k == 0)
        def _():
            to_relay(0).start()
            y_stage()

        @pl.when(k == 1)
        def _():
            to_relay(1).start()
            across_stage()

        for side in SIDES:
            for i in range(per):
                @pl.when(k == per * (1 + side) + i)
                def _(side=side, i=i):
                    to_side(i, side).start()

        @pl.when(k == 2)
        def _():
            to_relay(0).wait_recv()
            from_relay(0).start()

        @pl.when(k == 3)
        def _():
            to_relay(1).wait_recv()
            from_relay(1).start()

        @pl.when(k == 3)
        def _():
            x_stage((0, 1))

        @pl.when(k == 4)
        def _():
            x_stage((2,))

        @pl.when(k == 5)
        def _():
            d_stage((0, 1))

        @pl.when(k == 6)
        def _():
            d_stage((2,))

        for i in range(per):
            @pl.when(k == 3 * per + i)
            def _(i=i):
                ctx_ref[t, i] = ctx_buf[3 * per + i]

        return carry

    lax.fori_loop(0, seqs, body, 0)
    for which in range(3):
        for a in SIDES:
            wd(a, which).wait_recv()
    for side in SIDES:
        for i in range(per):
            to_side(i, side).wait_recv()
        from_relay(side).wait_recv()

    def finish():
        for side in SIDES:
            for i in range(per):
                to_side(i, side).wait_send()
            to_relay(side).wait_send()
            from_relay(side).wait_send()
        for a in SIDES:
            for side in SIDES:
                wy_own(a, side).wait_send()
            wy_forward(a).wait_send()
            for which in range(3):
                for side in SIDES:
                    wx_own(a, which, side).wait_send()
                wx_forward(a, which).wait_send()
                wd(a, which).wait_send()

    return finish


def cross_part(tp, ep, cap, experts, finish_self, ctx_ref, w_ref, wo_ref, pad_ref, gain_cross_ref, gain_ffn_ref, router_ref, idx_row_ref, y2_ref, send_ref, gate_ref, place_ref, dec_buf, enc_buf, y1_buf, x_buf, q_buf, kv_buf, acc_buf, y2_buf, route_buf, tri_buf, key_buf, kept_buf, idx_buf, choice_buf, gate_col, gate_out, gate_in, loads, y_send, y_recv, g_send, g_recv, out_sem):
    t, e = lax.axis_index('tp'), lax.axis_index('ep')
    right, left, across = lax.rem(t + 1, tp), lax.rem(t + tp - 1, tp), lax.rem(t + 2, tp)
    seqs, length, width = y2_buf.shape
    per = seqs // tp
    enc_len = enc_buf.shape[1]
    span = experts // ep
    share = span // tp
    chips = ep // 2
    wo_len = wo_ref.shape[1] // 2
    block = y1_buf.shape[0]
    halves = length // block

    def own(i, h, side):
        src = y2_buf.at[per * t + i, pl.ds(h * block, block)]
        return remote(src, src, y_send.at[side, i, h], y_recv.at[side, i, h], tp=(right, left)[side])

    def forward(side, h):
        src = y2_buf.at[per * (left, right)[side] + side, pl.ds(h * block, block)]
        return remote(src, src, y_send.at[2, side, h], y_recv.at[2, side, h], tp=(right, left)[side])

    def gates(side):
        return remote(gate_out, gate_in.at[side], g_send.at[side], g_recv.at[side], tp=(right, left, across)[side])

    def write(s):
        return pltpu.make_async_copy(y2_buf.at[s], y2_ref.at[s], out_sem.at[s])

    low = low_lanes(block)
    for copy in loads:
        copy.wait()

    def keys_values(row, carry):
        rest = dot_nt(enc_buf[ALL].reshape(per * enc_len, width), w_ref[row, WIDE:])
        for piece in range(3):
            kv_buf[row, piece] = rest[:, piece * LANES:(piece + 1) * LANES].astype(BF16)
        return carry

    lax.fori_loop(0, tp, keys_values, 0)
    def attend(step, carry):
        i, h = step // halves, lax.rem(step, halves)
        rows = pl.ds(pl.multiple_of(h * block, block), block)
        total = dec_buf[i, rows, :].astype(F32)
        for row in range(tp):
            total = total + (dot(ctx_ref[row, i, rows, :LANES], wo_ref[row, :LANES]) + dot(ctx_ref[row, i, rows, LANES:], wo_ref[row, wo_len - LANES:wo_len]))
        y1 = total.astype(BF16)
        y1_buf[ALL] = y1
        x_buf[ALL] = rms_norm(y1.astype(F32), gain_cross_ref[ALL])
        acc_buf[ALL] = jnp.zeros_like(acc_buf)
        pad_bias = jnp.where(pad_ref[pl.ds(per * t + i, 1), :] == 0, 0.0, NEG_LARGE)
        keys = pl.ds(pl.multiple_of(i * enc_len, enc_len), enc_len)

        def per_row(row, inner):
            pair = dot_nt(x_buf[ALL], w_ref[row, :WIDE])
            q01 = pair[:, :LANES]
            q_buf[0] = jnp.where(low, q01, 0.0).astype(BF16)
            q_buf[1] = jnp.where(low, 0.0, q01).astype(BF16)
            q_buf[2] = pair[:, LANES:].astype(BF16)
            mixed = []
            for head in range(3):
                key_at, value_at = (0, 1) if head < 2 else (2, 2)
                scores = dot_nt(q_buf[head], kv_buf[row, key_at, keys, :]) + pad_bias
                mixed.append(dot(softmax(scores), kv_buf[row, value_at, keys, :]))
            c01 = jnp.where(low, mixed[0], mixed[1]).astype(BF16)
            c2 = jnp.where(low, 0.0, mixed[2]).astype(BF16)
            acc_buf[ALL] += dot(c01, wo_ref[row, wo_len:wo_len + LANES]) + dot(c2, wo_ref[row, 2 * wo_len - LANES:])
            return inner

        lax.fori_loop(0, tp, per_row, 0)
        y2_buf[per * t + i, rows, :] = (y1_buf[ALL].astype(F32) + acc_buf[ALL]).astype(BF16)
        for at in range(per * halves):
            @pl.when(step == at)
            def _(at=at):
                for side in SIDES:
                    own(at // halves, at % halves, side).start()
        return carry

    lax.fori_loop(0, per * halves, attend, 0)

    w_full = router_ref[ALL]
    w_high = w_full.astype(BF16)
    w_rest = w_full - w_high.astype(F32)
    w_mid = w_rest.astype(BF16)
    route_buf[:, :experts] = w_high
    route_buf[:, experts:2 * experts] = w_mid
    route_buf[:, 2 * experts:] = (w_rest - w_mid.astype(F32)).astype(BF16)
    lane_e = lax.broadcasted_iota(jnp.int32, (length, experts), 1)
    lane_s = lax.broadcasted_iota(jnp.int32, choice_buf.shape, 1)
    idx_buf[ALL] = jnp.zeros_like(idx_buf)
    idx_buf[:seqs] = idx_row_ref[ALL].astype(F32)
    choice_buf[ALL] = idx_buf[ALL].T.astype(jnp.int32)
    gate_col[ALL] = jnp.zeros_like(gate_col)

    def own_gate(i, carry):
        s = per * t + i
        parts = dot(rms_norm(y2_buf[s].astype(F32), gain_ffn_ref[ALL]), route_buf[ALL])
        logits = parts[:, :experts] + (parts[:, experts:2 * experts] + parts[:, 2 * experts:])
        exps = jnp.exp(logits - jnp.max(logits, **ROW))
        choice = jnp.sum(jnp.where(lane_s == s, choice_buf[ALL], 0), **ROW)
        picked = jnp.sum(jnp.where(lane_e == choice, exps, 0.0), **ROW)
        gate_col[ALL] += jnp.where(lane_s == s, picked / jnp.sum(exps, **ROW), 0.0)
        return carry

    lax.fori_loop(0, per, own_gate, 0)
    idx_buf[ALL] = gate_col[ALL].T
    gate_out[ALL] = idx_buf[:seqs]
    for side in range(3):
        gates(side).start()

    row_ids = lax.broadcasted_iota(jnp.int32, (length, length), 0)
    col_ids = lax.broadcasted_iota(jnp.int32, (length, length), 1)
    tri_buf[ALL] = jnp.where(row_ids <= col_ids, 1.0, 0.0).astype(BF16)
    sub_e = lax.broadcasted_iota(jnp.int32, (experts, length), 0)
    first_rows = cap // 16 * 16
    rows2 = share // 2 * cap

    def place(s, base_col):
        row = idx_row_ref[pl.ds(s, 1), :]
        hot_t = jnp.where(sub_e == row, 1.0, 0.0)
        count_t = dot(hot_t.astype(BF16), tri_buf[ALL]) + base_col
        pos_t = jnp.sum(hot_t * count_t, axis=0, keepdims=True) - 1.0
        pos_i = pos_t.astype(jnp.int32)
        kept = pos_t < cap
        home, row_of, at = row // span, lax.rem(row // share, tp), lax.rem(row, share)
        key_buf[pl.ds(s, 1), :] = jnp.where(kept & (row_of == t), home * (share * cap) + at * cap + pos_i, -1)
        away = lax.rem(home // 2 - e // 2 + chips, chips)
        flip = lax.rem(home + e, 2)
        spot = jnp.where(away == 0, flip, jnp.where(away == 1, 2 + flip, jnp.where(away == 2, 6 + flip, 4 + flip)))
        half_share = share // 2
        q = lax.rem(at, half_share) * cap + pos_i
        inside = jnp.where(q < first_rows, spot * first_rows + q, ep * first_rows + spot * (rows2 - first_rows) + q - first_rows)
        where = (row_of * 2 + at // half_share) * (ep * rows2) + inside
        place_ref[pl.ds(s, 1), :] = jnp.where(kept, where * 8, 0)
        kept_buf[pl.ds(s, 1), :] = jnp.where(kept, 1.0, 0.0)
        return count_t[:, length - 1:]

    lax.fori_loop(0, seqs, place, jnp.zeros((experts, 1), F32))
    send_ref[ALL] = jnp.zeros_like(send_ref)
    chunk = send_ref.shape[0] // 2

    def consume(n, carry):
        near = jnp.where(lax.rem(n, 2) == 0, left, right)
        row = jnp.where(n < per, t, jnp.where(n < 3 * per, near, across))
        half = jnp.where(n < per, n, jnp.where(n < 3 * per, lax.rem(n // 2 + 1, 2), lax.rem(n, 2)))
        s = per * row + half

        @pl.when(n == 1)
        def _():
            for h in range(halves):
                own(0, h, 0).wait_recv()
                forward(0, h).start()

        @pl.when(n == 3)
        def _():
            for h in range(halves):
                own(0, h, 1).wait_recv()

        @pl.when(n == 4)
        def _():
            for h in range(halves):
                own(1, h, 1).wait_recv()
                forward(1, h).start()
            for h in range(halves):
                own(1, h, 0).wait_recv()

        for side in SIDES:
            @pl.when(n == 3 * per + side)
            def _(side=side):
                for h in range(halves):
                    forward(side, h).wait_recv()

        write(s).start()

        key = key_buf[pl.ds(s, 1), :]

        def dispatch(d, inner):
            rows = pl.ds(pl.multiple_of(d * chunk, chunk), chunk)
            hot = jnp.where(lax.broadcasted_iota(jnp.int32, (chunk, length), 0) + d * chunk == key, 1.0, 0.0).astype(BF16)
            send_ref[rows, :] = (send_ref[rows, :].astype(F32) + dot(hot, y2_buf[s])).astype(BF16)
            return inner

        lax.fori_loop(0, 2, dispatch, 0)
        return carry

    lax.fori_loop(0, seqs, consume, 0)
    finish_self()
    for side in range(3):
        gates(side).wait()
    gate_ref[ALL] = (gate_out[ALL] + gate_in[0] + gate_in[1] + gate_in[2]) * kept_buf[ALL]
    for s in range(seqs):
        write(s).wait()
    for side in SIDES:
        for h in range(halves):
            for i in range(per):
                own(i, h, side).wait_send()
            forward(side, h).wait_send()


def attention_kernel(tp, ep, cap, experts, dec_ref, enc_ref, pad_ref, idx_ref, bias_ref, gain_self, gain_cross, gain_ffn, router_ref, wq_self, wk_self, wv_self, wo_self, wq_cross, wk_cross, wv_cross, wo_cross, y2_ref, send_ref, gate_ref, place_ref, ctx_all, w_all, wo_all, dec_pair, head_buf, ctx_buf, relay, w_ref, dec_buf, enc_buf, y1_buf, x_buf, q_buf, kv_buf, acc_buf, y2_buf, route_buf, tri_buf, key_buf, kept_buf, idx_buf, choice_buf, gate_col, gate_out, gate_in, dec_sem, ctx_send, ctx_recv, wy_send, wy_recv, wx_send, wx_recv, wd_send, wd_recv, load_sem, y_send, y_recv, g_send, g_recv, out_sem):
    per = dec_buf.shape[0]
    t = lax.axis_index('tp')
    finish_self = self_part(tp, ep, dec_ref, gain_self, bias_ref, wq_self, wk_self, wv_self, wo_self, wq_cross, wk_cross, wv_cross, wo_cross, ctx_all, w_all, wo_all, dec_pair, head_buf, ctx_buf, relay, w_ref, dec_sem, ctx_send, ctx_recv, wy_send, wy_recv, wx_send, wx_recv, wd_send, wd_recv)
    loads = [
        pltpu.make_async_copy(enc_ref.at[pl.ds(per * t, per)], enc_buf, load_sem.at[0]),
        pltpu.make_async_copy(dec_ref.at[pl.ds(per * t, per)], dec_buf, load_sem.at[1]),
    ]
    for copy in loads:
        copy.start()
    cross_part(tp, ep, cap, experts, finish_self, ctx_all, w_all, wo_all, pad_ref, gain_cross, gain_ffn, router_ref, idx_ref, y2_ref, send_ref, gate_ref, place_ref, dec_buf, enc_buf, y1_buf, x_buf, q_buf, kv_buf, acc_buf, y2_buf, route_buf, tri_buf, key_buf, kept_buf, idx_buf, choice_buf, gate_col, gate_out, gate_in, loads, y_send, y_recv, g_send, g_recv, out_sem)


def expert_kernel(tp, ep, cap, send_ref, w_in_ref, w_out_ref, gain_ref, all_hbm, all_ref, got, relay, staged, acc_buf, out_stage, out_buf, back, w_in_buf, w_out_buf, xd_send, xd_recv, xr_send, xr_recv, y_send, y_recv, w_sem, own_sem, out_sem):
    t, e = lax.axis_index('tp'), lax.axis_index('ep')
    right, left, across = lax.rem(t + 1, tp), lax.rem(t + tp - 1, tp), lax.rem(t + 2, tp)
    chips = ep // 2
    core, x = lax.rem(e, 2), e // 2
    share, _, width = staged.shape
    ff = w_in_buf.shape[2]
    rows2 = 2 * cap
    over, under = (cap + 15) // 16 * 16, cap // 16 * 16
    in_at = tuple(j // 2 * rows2 + j % 2 * over for j in range(share))
    in_len = tuple((rows2 - over) if j % 2 else over for j in range(share))
    out_at = tuple(j // 2 * rows2 + j % 2 * under for j in range(share))
    out_len = tuple((rows2 - under) if j % 2 else under for j in range(share))

    def inn(j):
        return pl.ds(in_at[j], in_len[j])

    def out(j):
        return pl.ds(out_at[j], out_len[j])

    def region(j, n, count=1):
        return pl.ds(out_at[j] * ep + n * out_len[j], count * out_len[j])

    def member(dx, flip):
        return 2 * lax.rem(x + dx + chips, chips) + (core if flip == 0 else 1 - core)

    near = {1: (0, 1), 2: (1, 0), 3: (1, 1), 4: (-1, 0), 5: (-1, 1)}
    x_right, x_left = member(1, 0), member(-1, 0)
    friends = [{'tp': right}, {'tp': left}] + [{'ep': member(*near[n])} for n in near]
    greet(friends)

    def to(n):
        return member(*near[n])

    def origin(n):
        return e if n == 0 else member(-near[n][0], near[n][1]) if n in near else member(2, n - 6)

    def dispatch(n, j):
        return remote(send_ref.at[to(n), inn(j)], got.at[n, inn(j)], xd_send.at[n, j], xd_recv.at[n, j], ep=to(n))

    def dispatch_via(side, j):
        return remote(send_ref.at[member(2, side), inn(j)], relay.at[side, inn(j)], xd_send.at[6 + side, j], xd_recv.at[6 + side, j], ep=(x_right, x_left)[side])

    def dispatch_on(side, j):
        return remote(relay.at[side, inn(j)], got.at[6 + side, inn(j)], xd_send.at[8 + side, j], xd_recv.at[8 + side, j], ep=(x_right, member(-1, 1))[side])

    def give(n, j):
        return remote(out_buf.at[n, out(j)], all_ref.at[t, region(j, n)], xr_send.at[n, j], xr_recv.at[n, j], ep=origin(n))

    def give_via(side, j):
        return remote(out_buf.at[6 + side, out(j)], back.at[side, out(j)], xr_send.at[6 + side, j], xr_recv.at[6 + side, j], ep=(x_right, x_left)[side])

    def give_on(side, j):
        return remote(back.at[side, out(j)], all_ref.at[t, region(j, 6 + side)], xr_send.at[8 + side, j], xr_recv.at[8 + side, j], ep=(x_right, member(-1, 1))[side])

    def own_dispatch(j):
        return pltpu.make_async_copy(send_ref.at[e, inn(j)], got.at[0, inn(j)], own_sem.at[0, j])

    def write(r, j):
        row = (t, left, right, across)[r]
        return pltpu.make_async_copy(all_ref.at[row, region(j, 0, ep)], all_hbm.at[row, region(j, 0, ep)], out_sem.at[r, j])

    def weights(j):
        return (pltpu.make_async_copy(w_in_ref.at[share * t + j], w_in_buf.at[j], w_sem.at[0, j]), pltpu.make_async_copy(w_out_ref.at[share * t + j], w_out_buf.at[j], w_sem.at[1, j]))

    def dispatch_all(j):
        for side in SIDES:
            dispatch_via(side, j).start()
        for n in (2, 4, 3, 5, 1):
            dispatch(n, j).start()
        own_dispatch(j).start()

    def unpack(n, j):
        start = j // 2 * rows2 + (under if j % 2 else 0)
        block = got[n, start:start + over].astype(F32)
        block = block[over - cap:] if j % 2 else block[:cap]
        staged[j, n * cap:(n + 1) * cap, :] = rms_norm(block, gain_ref[ALL]).astype(F32)

    def run_expert(j):
        for copy in weights(j):
            copy.wait()
        inputs = staged[j].astype(BF16)

        def ffn(c, carry):
            cols = pl.ds(pl.multiple_of(c * width, LANES), width)
            hidden = jnp.maximum(dot(inputs, w_in_buf[j, :, cols]), 0.0).astype(BF16)
            acc = dot(hidden, w_out_buf[j, cols, :])

            @pl.when(c == 0)
            def _():
                acc_buf[j % 2] = acc

            @pl.when(c > 0)
            def _():
                acc_buf[j % 2] += acc

            return carry

        lax.fori_loop(0, ff // width, ffn, 0)

    def repack(n, j):
        start = n * cap
        if j % 2 == 0:
            out_buf[n, out_at[j]:out_at[j] + under] = acc_buf[0, start:start + under].astype(BF16)
        else:
            out_stage[:cap - under] = acc_buf[0, start + under:start + cap]
            out_stage[cap - under:] = acc_buf[1, start:start + cap]
            out_buf[n, out_at[j]:out_at[j] + out_len[j]] = out_stage[ALL].astype(BF16)

    def dispatch_forward(j):
        for side in SIDES:
            dispatch_via(side, j).wait_recv()
            dispatch_on(side, j).start()

    def forward_back(j):
        for side in SIDES:
            give_via(side, j).wait_recv()
            give_on(side, j).start()

    def take(j):
        own_dispatch(j).wait()
        unpack(0, j)
        for n in (1, 2, 4, 3, 5):
            dispatch(n, j).wait_recv()
            unpack(n, j)
        for side in SIDES:
            dispatch_on(side, j).wait_recv()
            unpack(6 + side, j)

    def give_all(j):
        for n in (6, 7, 2, 4, 3, 5, 1, 0):
            repack(n, j)
            if n >= 6:
                give_via(n - 6, j).start()
            elif n > 0:
                give(n, j).start()
            else:
                all_ref[t, region(j, 0)] = out_buf[0, out_at[j]:out_at[j] + out_len[j]]

    parts = ((0, 2), (2, 4), (6, 2))

    def share_out(c, j, side):
        src = all_ref.at[t, region(j, *parts[c])]
        return remote(src, src, y_send.at[side, c, j], y_recv.at[side, c, j], tp=(right, left)[side])

    def pass_on(side, j):
        src = all_ref.at[(left, right)[side], region(j, side * chips, chips)]
        return remote(src, src, y_send.at[2, side, j], y_recv.at[2, side, j], tp=(right, left)[side])

    def broadcast(j, chosen=(0, 1, 2)):
        for c in chosen:
            for n in ((0, 1), (2, 4, 3, 5), (6, 7))[c]:
                if 0 < n < 6:
                    give(n, j).wait_recv()
                elif n >= 6:
                    give_on(n - 6, j).wait_recv()
            for side in SIDES:
                share_out(c, j, side).start()

    def relay_out(j):
        for c in SIDES:
            for side in SIDES:
                share_out(c, j, side).wait_recv()
        pass_on(0, j).start()
        for side in SIDES:
            share_out(2, j, side).wait_recv()
        pass_on(1, j).start()
        for r in range(3):
            write(r, j).start()

    def collect(j):
        for side in SIDES:
            pass_on(side, j).wait_recv()
        write(3, j).start()

    def fetch(j):
        for copy in weights(j):
            copy.start()

    def early(j):
        broadcast(j, SIDES)

    def late(j):
        broadcast(j, (len(parts) - 1,))

    a, b, c, d = range(share)
    fetch(a)
    meet(friends)
    for j in (a, b, c, d):
        dispatch_all(j)
    for j in (b, c, d):
        fetch(j)
    dispatch_forward(a)
    take(a)
    run_expert(a)
    dispatch_forward(b)
    dispatch_forward(c)
    give_all(a)
    take(b)
    run_expert(b)
    dispatch_forward(d)
    forward_back(a)
    give_all(b)
    early(a)
    take(c)
    run_expert(c)
    forward_back(b)
    late(a)
    give_all(c)
    early(b)
    relay_out(a)
    take(d)
    run_expert(d)
    late(b)
    forward_back(c)
    give_all(d)
    early(c)
    late(c)
    relay_out(b)
    forward_back(d)
    early(d)
    late(d)
    relay_out(c)
    collect(a)
    collect(b)
    relay_out(d)
    collect(c)
    collect(d)
    for j in range(share):
        for side in SIDES:
            pass_on(side, j).wait_send()
            for c in range(len(parts)):
                share_out(c, j, side).wait_send()
            dispatch_via(side, j).wait_send()
            dispatch_on(side, j).wait_send()
            give_via(side, j).wait_send()
            give_on(side, j).wait_send()
        for n in near:
            dispatch(n, j).wait_send()
            give(n, j).wait_send()
        for r in range(tp):
            write(r, j).wait()


def combine_kernel(place_ref, all_ref, y2_ref, gate_ref, out_ref, raw, wide, picked, gate_pad, gate_col, raw_sem):
    s = pl.program_id(0)
    blocks, rows, width = raw.shape
    tiles = width // LANES
    length = picked.shape[0] // 8

    @pl.when(s == 0)
    def _():
        def load(b):
            return pltpu.make_async_copy(all_ref.at[b], raw.at[b], raw_sem.at[b])

        for b in range(blocks):
            load(b).start()
        gate_pad[ALL] = jnp.zeros_like(gate_pad)
        gate_pad[:gate_ref.shape[0]] = gate_ref[ALL]
        gate_col[ALL] = gate_pad[ALL].T

        def spread(b, carry):
            load(b).wait()

            def part(i, inner):
                values = raw[b, pl.ds(pl.multiple_of(i * 16, 16), 16), :].astype(F32)
                start = pl.multiple_of((b * rows + i * 16) * 8, LANES)
                for j in range(tiles):
                    wide[pl.ds(start + j, 16, stride=8), :] = values[:, j * LANES:(j + 1) * LANES]
                return inner

            lax.fori_loop(0, rows // 16, part, 0, unroll=4)
            return carry

        lax.fori_loop(0, blocks, spread, 0)

    def pick(i, carry):
        for u in range(16):
            token = i * 16 + u
            start = pl.multiple_of(place_ref[s, token], 8)
            picked[pl.ds(pl.multiple_of(token * 8, 8), 8), :] = wide[pl.ds(start, 8), :]
        return carry

    lax.fori_loop(0, length // 16, pick, 0)
    lane_s = lax.broadcasted_iota(jnp.int32, gate_col.shape, 1)
    gate = jnp.sum(jnp.where(lane_s == s, gate_col[ALL], 0.0), **ROW)
    for j in range(tiles):
        cols = slice(j * LANES, (j + 1) * LANES)
        out_ref[0, :, cols] = (y2_ref[0, :, cols].astype(F32) + gate * picked[pl.ds(j, length, stride=8), :]).astype(BF16)


def any_spec():
    return pl.BlockSpec(memory_space=pl.ANY)


def vmem_spec():
    return pl.BlockSpec(memory_space=pltpu.VMEM)


def params(number):
    return pltpu.CompilerParams(collective_id=number, has_side_effects=True, vmem_limit_bytes=VMEM_LIMIT)


def solution(mesh):
    tp, ep = mesh.shape['tp'], mesh.shape['ep']
    dma = pltpu.SemaphoreType.DMA
    token_spec = P(('part', 'ep'), None, None)
    row_spec = P(('part', 'ep'), None)
    col_spec = P(None, 'tp')
    head_rows = P('tp', None)
    vec_spec = P(None)
    expert_spec = P('ep', None, None)
    in_specs = (token_spec, token_spec, row_spec, row_spec, P('tp', None, None), vec_spec, col_spec, col_spec, col_spec, head_rows, vec_spec, col_spec, col_spec, col_spec, head_rows, vec_spec, P(None, None), expert_spec, expert_spec)

    def layer(dec_states, enc_states, enc_pad, expert_idx, self_bias, gain_self, wq_self, wk_self, wv_self, wo_self, gain_cross, wq_cross, wk_cross, wv_cross, wo_cross, gain_ffn, w_router, w_in, w_out):
        seqs, length, width = dec_states.shape
        enc_len = enc_states.shape[1]
        per = seqs // tp
        experts = w_router.shape[1]
        tokens = seqs * length
        cap = (5 * tokens + 4 * experts - 1) // (4 * experts)
        share = experts // ep // tp
        two, six = dma((2,)), dma((2, 3))
        packed, out_rows = 5 * LANES, 2 * wo_self.shape[0]
        y2, send, gate, place = pl.pallas_call(
            functools.partial(attention_kernel, tp, ep, cap, experts),
            name='attention',
            out_shape=(
                jax.ShapeDtypeStruct((seqs, length, width), BF16),
                jax.ShapeDtypeStruct((ep * share * cap, width), BF16),
                jax.ShapeDtypeStruct((seqs, length), F32),
                jax.ShapeDtypeStruct((seqs, length), jnp.int32),
            ),
            in_specs=[any_spec(), any_spec()] + [vmem_spec()] * 15,
            out_specs=(any_spec(), vmem_spec(), vmem_spec(), vmem_spec()),
            scratch_shapes=[
                pltpu.VMEM((tp, per, length, WIDE), BF16),
                pltpu.VMEM((tp, packed, width), BF16),
                pltpu.VMEM((tp, out_rows, width), BF16),
                pltpu.VMEM((2, length, width), BF16),
                pltpu.VMEM((6, length, LANES), BF16),
                pltpu.VMEM((seqs, length, WIDE), BF16),
                pltpu.VMEM((2, length, WIDE), BF16),
                pltpu.VMEM((packed, width), BF16),
                pltpu.VMEM((per, length, width), BF16),
                pltpu.VMEM((per, enc_len, width), BF16),
                pltpu.VMEM((length // 2, width), BF16),
                pltpu.VMEM((length // 2, width), BF16),
                pltpu.VMEM((3, length // 2, LANES), BF16),
                pltpu.VMEM((tp, 3, per * enc_len, LANES), BF16),
                pltpu.VMEM((length // 2, width), F32),
                pltpu.VMEM((seqs, length, width), BF16),
                pltpu.VMEM((width, 3 * experts), BF16),
                pltpu.VMEM((length, length), BF16),
                pltpu.VMEM((seqs, length), jnp.int32),
                pltpu.VMEM((seqs, length), F32),
                pltpu.VMEM((LANES, length), F32),
                pltpu.VMEM((length, LANES), jnp.int32),
                pltpu.VMEM((length, LANES), F32),
                pltpu.VMEM((seqs, length), F32),
                pltpu.VMEM((3, seqs, length), F32),
                two, *[dma((4, 2))] * 2, *[six] * 2, *[dma((2, 3, 3))] * 2, *[six] * 2, two, *[dma((3, per, 2))] * 2, *[dma((3,))] * 2, dma((seqs,)),
            ],
            compiler_params=params(0),
        )(dec_states, enc_states, enc_pad, expert_idx, self_bias, gain_self, gain_cross, gain_ffn, w_router, wq_self.T, wk_self.T, wv_self.T, wo_self, wq_cross.T, wk_cross.T, wv_cross.T, wo_cross)
        ff = w_in.shape[2]
        rows = share * cap
        expert_out = pl.pallas_call(
            functools.partial(expert_kernel, tp, ep, cap),
            name='experts',
            out_shape=jax.ShapeDtypeStruct((tp, ep * rows, width), BF16),
            in_specs=[any_spec(), any_spec(), any_spec(), vmem_spec()],
            out_specs=any_spec(),
            scratch_shapes=[
                pltpu.VMEM((tp, ep * rows, width), BF16),
                pltpu.VMEM((ep, rows, width), BF16),
                pltpu.VMEM((2, rows, width), BF16),
                pltpu.VMEM((share, ep * cap, width), F32),
                pltpu.VMEM((2, ep * cap, width), F32),
                pltpu.VMEM((2 * cap - cap // 16 * 16, width), F32),
                pltpu.VMEM((ep, rows, width), BF16),
                pltpu.VMEM((2, rows, width), BF16),
                pltpu.VMEM((share, width, ff), BF16),
                pltpu.VMEM((share, ff, width), BF16),
                *[dma((ep + 2, share))] * 4, *[dma((3, 3, share))] * 2, *[dma((2, share))] * 2, dma((tp, share)),
            ],
            compiler_params=params(2),
        )(send.reshape(ep, rows, width), w_in, w_out, gain_ffn)
        slots = tp * ep * rows
        blocks = 2 * tp
        return pl.pallas_call(
            combine_kernel,
            name='combine',
            grid=(seqs,),
            out_shape=jax.ShapeDtypeStruct((seqs, length, width), BF16),
            in_specs=[
                pl.BlockSpec(memory_space=pltpu.SMEM),
                any_spec(),
                pl.BlockSpec((1, length, width), lambda s: (s, 0, 0)),
                vmem_spec(),
            ],
            out_specs=pl.BlockSpec((1, length, width), lambda s: (s, 0, 0)),
            scratch_shapes=[
                pltpu.VMEM((blocks, slots // blocks, width), BF16),
                pltpu.VMEM((slots * 8, LANES), F32),
                pltpu.VMEM((length * 8, LANES), F32),
                pltpu.VMEM((LANES, length), F32),
                pltpu.VMEM((length, LANES), F32),
                dma((blocks,)),
            ],
            compiler_params=pltpu.CompilerParams(vmem_limit_bytes=VMEM_LIMIT),
        )(place, expert_out.reshape(blocks, slots // blocks, width), y2, gate)

    return jax.shard_map(layer, mesh=mesh, in_specs=in_specs, out_specs=token_spec, check_vma=False)
```

time: 731 us -> 246 us (0.34); the launches traced: 723 us -> 246 us
  waiting for transfers between devices: 298 us -> 0 us
  Pallas kernels: 0 us -> 246 us
  matrix products: 245 us -> 0 us
  blocking collectives: 93.2 us -> 0 us
  other arithmetic: 50.7 us -> 0 us
  local copies, waits for them, and re-layouts: 14.4 us -> 0 us
  between operations: 14.2 us -> 0.18 us
    pallas_call x0 -> x3, Pallas kernels: none -> 246 us  [the longest x1 120 us: layer(): pl.pallas_call(functools.partial(attention_kernel, tp, ep, cap, experts),...]
    dot_general x13 -> x0, matrix products: 220 us -> none  [the longest x1 42.4 us: expert_layer(): jnp.einsum('sc,sd->cd', dispatch, normed, preferred_element_type=jnp.floa...]
    psum x2 -> x0, waiting for transfers between devices: 220 us -> none  [layer(): attn_sum = lax.psum(partial.astype(jnp.bfloat16), 'tp')]
    all_to_all x1 -> x0, blocking collectives: 93.2 us -> none  [expert_layer(): lax.all_to_all(send_buf.reshape(experts, capacity, d_model), 'ep', 0, 0,...]
    all_to_all x1 -> x0, waiting for transfers between devices: 78.6 us -> none  [expert_layer(): lax.all_to_all(expert_out.reshape(experts, capacity, d_model), 'ep', 0, 0...]
    sub x2 -> x0, matrix products: 25 us -> none  [attention_heads(): weights = jax.nn.softmax(scores, axis=-1).astype(jnp.bfloat16)]
    reduce_sum x6 -> x0, other arithmetic: 23.5 us -> none  [the longest x3 20.6 us: rms_norm(): mean_sq = jnp.mean(upcast * upcast, axis=-1, keepdims=True)]
    dot_general x1 -> x0, other arithmetic: 14.5 us -> none  [expert_layer(): jnp.einsum('sc,sd->cd', dispatch, normed, preferred_element_type=jnp.floa...]
  transfers between devices with their start and end apart: 3 -> 0, of which waited for: 3 -> 0; matrix products, arithmetic and copies ran while one was open for 5% -> 0% of each run, Pallas kernels for 0% -> 0%
where the time goes in v2:
time: 246 us
  Pallas kernels  246 us (100%)
    pallas_call x1, Pallas kernels, layer(): pl.pallas_call(functools.partial(attention_kernel, tp, ep, cap, experts),...  120 us
    pallas_call x1, Pallas kernels, layer(): pl.pallas_call(functools.partial(expert_kernel, tp, ep, cap), name='exper...  105 us
    pallas_call x1, Pallas kernels, layer(): pl.pallas_call(combine_kernel, name='combine', grid=(seqs,), out_shape=ja...  21 us

profile of v2, /device:TPU:97, one launch (start us, length us, event | category | flops | bytes accessed | tf_op | source)
XLA Modules:
  0.0 246.0 jit_solution(17364862017181396765)
XLA Ops:
  0.0 120.1 %attention.1 = (bf16[8,512,768]{2,1,0:T(8,128)(2,1)}, bf16[1280,768]{1,0:T(8,128)(2,1)}, f32[8,512]{1,0:T(8,128)}, s32[8,512]{1,0:T(8,128)}) custom-call(bf16[8,512,768]{2,1,0:T(8,128)(2,1)} %dec_ref.1, bf16[8,256,768]{2,1,0:T(8,128)(2,1)} %enc_ref.1, s32[8,256]{1,0:T(8,128)} %pad_ref.1, s32[8,512]{1,0:T(8,128)} %idx_ref.1, f32[3,512,512]{2,1,0:T(8,128)} %bias_ref.1, ...), custom_call_target="tpu_custom_call" | custom-call | tf_op jit(solution)/shard_map/attention/pallas_call | solution.py:809
  120.1 104.8 %experts.1 = bf16[4,1280,768]{2,1,0:T(8,128)(2,1)} custom-call(bf16[8,160,768]{2,1,0:T(8,128)(2,1)} %bitcast.9, bf16[16,768,3072]{2,1,0:T(8,128)(2,1)} %w_in_ref.1, bf16[16,3072,768]{2,1,0:T(8,128)(2,1)} %w_out_ref.1, f32[768]{0:T(1024)} %gain_ref.1), custom_call_target="tpu_custom_call" | custom-call | tf_op jit(solution)/shard_map/experts/pallas_call | solution.py:852
  224.8 21.0 %combine.1 = bf16[8,512,768]{2,1,0:T(8,128)(2,1)} custom-call(s32[8,512]{1,0:T(8,128)} %get-tuple-element.9.place_ref, bf16[8,640,768]{2,1,0:T(8,128)(2,1)} %bitcast.8, bf16[8,512,768]{2,1,0:T(8,128)(2,1)} %get-tuple-element.11.y2_ref, f32[8,512]{1,0:T(8,128)} %get-tuple-element.12.gate_ref), custom_call_target="tpu_custom_call" | custom-call | tf_op jit(solution)/shard_map/combine/pallas_call | solution.py:875
